TPU v7x, 32 devices: a whole 2x2x4 slice. The times are simulated.
32 devices in a mesh: gx: 4 (over z), gy: 8 (over y, x, core).
Axes of the slice: x: 2, y: 2, z: 4, core: 2. Of those that a mesh axis runs over, the one named last changes fastest.
Arguments:
- atm_members: float32 [4, 8, 80, 12, 128], P('gx', 'gy'), may hold values from -6 to 6
- ocean_members: bfloat16 [4, 8, 80, 1024], P('gx', 'gy'), may hold values from -6 to 6
- remap_weights: bfloat16 [4, 8, 4, 1024, 128], P('gx', 'gy'), may hold values from -0.09375 to 0.09375
- pair_src: int32 [4, 8, 4], P('gx', 'gy'), may hold values from 0 to 31, as said below
- obs_cell: int32 [4, 8, 64], P('gx', 'gy'), may hold values from 0 to 127
- obs_value: float32 [4, 8, 64], P('gx', 'gy'), may hold values from -8 to 8
- obs_error: float32 [4, 8, 64], P('gx', 'gy'), may hold values from 2 to 16
- obs_live: int32 [4, 8, 64], P('gx', 'gy'), may hold values from 0 to 1, as said below
- obs_order: int32 [4, 8, 64], P('gx', 'gy'), may hold values from 0 to 63, each once within a row
Outputs:
- post_mean: float32 [4, 8, 13, 128], P('gx', 'gy')
- post_anom: float32 [4, 8, 80, 13, 128], P('gx', 'gy')
Inputs may be any that keep to these rules, and one draw needn't show every extreme that they name: `pair_src`: for atmosphere tile (i, j) the 4 numbers are distinct, each a * 8 + b with |a - i| <= 1 and |b - j| <= 1. `obs_live`: the live slots of a tile are its first ones, between 8 and 64 of them; some tile has all slots live. `obs_order`: each tile's last dimension is a permutation of its slots.
All inputs are finite; a program needn't handle non-finite values.
Results may differ from a plain program's by a relative error of at most 0.0003.
Values may be sent and summed in bfloat16 or wider, within the bound.
A program may use at most 64 MiB of HBM per device.

v0:
```python
import jax
import jax.numpy as jnp
from jax import lax
from jax.sharding import PartitionSpec as P

MEM = 80
AX = 8
AY = 16
OCN_DEV = 1024
OB = 32
NB = 2
K = 4
FIELDS = 12
CELLS = 128
RAD = 2


exact_mode = lax.Precision.HIGHEST


def extended(block, sides, width):
    for axis, dim in sides:
        count = lax.axis_size(axis)
        forward = [(i, i + 1) for i in range(count - 1)]
        backward = [(target, source) for source, target in forward]
        low = lax.ppermute(
            lax.slice_in_dim(block, block.shape[dim] - width, None, axis=dim), axis, forward
        )
        high = lax.ppermute(lax.slice_in_dim(block, 0, width, axis=dim), axis, backward)
        block = jnp.concatenate([low, block, high], axis=dim)
    return block


def update_group(packets, anomaly, base_x, base_y):
    members = anomaly.shape[0]
    components = anomaly.shape[1]
    cell_count = anomaly.shape[2]
    observed = jnp.transpose(packets[:, :members, :], (1, 0, 2)).reshape(members, -1)
    innovation = packets[:, members, :].reshape(-1)
    errors = packets[:, members + 1, :].reshape(-1)
    obs_x = packets[:, members + 2, :].reshape(-1)
    obs_y = packets[:, members + 3, :].reshape(-1)
    live = packets[:, members + 4, :].reshape(-1)
    variance = jnp.sum(observed * observed, axis=0) / (members - 1)
    denominator = variance + errors + (1.0 - live)
    weighting = live / denominator
    damping = 1.0 / (1.0 + jnp.sqrt(errors / denominator))
    cell_index = jnp.arange(cell_count, dtype=jnp.int32)
    cell_x = (base_x + cell_index // AY).astype(jnp.float32)
    cell_y = (base_y + cell_index % AY).astype(jnp.float32)
    distance = (obs_x[:, None] - cell_x[None, :]) ** 2 + (obs_y[:, None] - cell_y[None, :]) ** 2
    taper = jnp.maximum(1.0 - distance / float(RAD * RAD), 0.0) ** 2
    flat_anomaly = anomaly.reshape(members, components * cell_count)
    covariance = jnp.dot(
        observed.T, flat_anomaly, precision=exact_mode, preferred_element_type=jnp.float32
    ) / (members - 1)
    gain = covariance.reshape(-1, components, cell_count) * (taper * weighting[:, None])[:, None, :]
    gain = gain.reshape(-1, components * cell_count)
    mean_step = jnp.dot(
        innovation[None, :], gain, precision=exact_mode, preferred_element_type=jnp.float32
    )
    anomaly_step = jnp.dot(
        observed * damping[None, :], gain, precision=exact_mode, preferred_element_type=jnp.float32
    )
    return (
        mean_step.reshape(components, cell_count),
        anomaly_step.reshape(members, components, cell_count),
    )


def local(
    atm_members,
    ocean_members,
    remap_weights,
    pair_src,
    obs_cell,
    obs_value,
    obs_error,
    obs_live,
    obs_order,
):
    sources = pair_src[0, 0]
    weights = remap_weights[0, 0].reshape(K * OCN_DEV, CELLS)
    row_count = lax.axis_size("gy")
    position = (sources // row_count - lax.axis_index("gx") + 1) * 3 + (
        sources % row_count - lax.axis_index("gy") + 1
    )
    column = extended(ocean_members, (("gx", 0),), 1)
    nearby_rows = extended(column, (("gy", 1),), 1)
    flattened = nearby_rows.reshape(9, MEM * OCN_DEV)
    selector = (position[:, None] == jnp.arange(9, dtype=jnp.int32)[None, :]).astype(jnp.bfloat16)
    chosen = jnp.dot(selector, flattened, preferred_element_type=jnp.float32)
    chosen = chosen.astype(jnp.bfloat16)
    stacked = jnp.transpose(chosen.reshape(K, MEM, OCN_DEV), (1, 0, 2)).reshape(MEM, K * OCN_DEV)
    surface = jnp.dot(stacked, weights, preferred_element_type=jnp.float32)
    state = jnp.concatenate([atm_members[0, 0], surface[:, None, :]], axis=1)
    ens_mean = jnp.sum(state, axis=0) / MEM
    anomaly = state - ens_mean[None]
    base_x = lax.axis_index("gx") * AX
    base_y = lax.axis_index("gy") * AY
    for batch_index in range(NB):
        obs_slots = obs_order[0, 0, batch_index * OB : (batch_index + 1) * OB]
        obs_cells = obs_cell[0, 0][obs_slots]
        observed = anomaly[:, FIELDS, :][:, obs_cells]
        predicted = ens_mean[FIELDS][obs_cells]
        innovation = obs_value[0, 0][obs_slots] - predicted
        errors = obs_error[0, 0][obs_slots]
        pos_x = (base_x + obs_cells // AY).astype(jnp.float32)
        pos_y = (base_y + obs_cells % AY).astype(jnp.float32)
        live = obs_live[0, 0][obs_slots].astype(jnp.float32)
        extras = jnp.stack([innovation, errors, pos_x, pos_y, live], axis=0)
        packet = jnp.concatenate([observed, extras], axis=0)[None, None]
        nearby = extended(packet, (("gx", 0), ("gy", 1)), 1)
        mean_total = jnp.zeros_like(ens_mean)
        anomaly_total = jnp.zeros_like(anomaly)
        for row_index in range(3):
            mean_step, anomaly_step = update_group(nearby[row_index], anomaly, base_x, base_y)
            mean_total = mean_total + mean_step
            anomaly_total = anomaly_total + anomaly_step
        ens_mean = ens_mean + mean_total
        anomaly = anomaly - anomaly_total
    return (ens_mean[None, None], anomaly[None, None])


def solution(mesh):
    in_specs = (
        P("gx", "gy", None, None, None),
        P("gx", "gy", None, None),
        P("gx", "gy", None, None, None),
        P("gx", "gy", None),
        P("gx", "gy", None),
        P("gx", "gy", None),
        P("gx", "gy", None),
        P("gx", "gy", None),
        P("gx", "gy", None),
    )
    out_specs = (P("gx", "gy", None, None), P("gx", "gy", None, None, None))
    return jax.shard_map(local, mesh=mesh, in_specs=in_specs, out_specs=out_specs, check_vma=False)
```

profile of v0, /device:TPU:3, one launch (start us, length us, event | category | flops | bytes accessed | tf_op | source)
XLA Modules:
  0.0 100.0 jit_solution(7388722212794545580)
XLA Ops:
  0.7 3.3 %collective-permute-start = (bf16[1,1,80,1024]{3,2,1,0:T(8,128)(2,1)}, bf16[1,1,80,1024]{3,2,1,0:T(8,128)(2,1)S(1)}, u32[]{:S(2)}, u32[]{:S(2)}) collective-permute-start(bf16[1,1,80,1024]{3,2,1,0:T(8,128)(2,1)} %param.10), channel_id=1, source_target_pairs={{0,8},{8,16},{16,24},{1,9},{9,17},{17,25},{2,10},{10,18},{18,26},{... | collective-permute-start | bytes 491528 | tf_op jit(solution)/shard_map/ppermute | solution.py:26
  4.0 1.3 %collective-permute-start.1 = (bf16[1,1,80,1024]{3,2,1,0:T(8,128)(2,1)}, bf16[1,1,80,1024]{3,2,1,0:T(8,128)(2,1)S(1)}, u32[]{:S(2)}, u32[]{:S(2)}) collective-permute-start(bf16[1,1,80,1024]{3,2,1,0:T(8,128)(2,1)} %param.10), channel_id=1, source_target_pairs={{8,0},{16,8},{24,16},{9,1},{17,9},{25,17},{10,2},{18,10},{26,18},{... | collective-permute-start | bytes 491528 | tf_op jit(solution)/shard_map/ppermute | solution.py:29
  6.1 1.4 %gather_fusion = s32[32]{0:T(128)S(1)} fusion(s32[64]{0:T(128)} %bitcast.290, s32[1024]{0:T(1024)S(1)} %get-tuple-element.69), kind=kCustom, calls=%fused_computation | custom fusion | bytes 384 | tf_op jit(solution)/shard_map/gather | solution.py:103
  7.5 1.4 %gather_fusion.5 = s32[32]{0:T(128)S(1)} fusion(s32[64]{0:T(128)} %bitcast.292, s32[1024]{0:T(1024)S(1)} %get-tuple-element.69), kind=kCustom, calls=%fused_computation.5 | custom fusion | bytes 384 | tf_op jit(solution)/shard_map/gather | solution.py:110
  8.9 1.4 %gather_fusion.6 = s32[32]{0:T(128)S(1)} fusion(s32[64]{0:T(128)} %bitcast.291, s32[1024]{0:T(1024)S(1)} %get-tuple-element.68), kind=kCustom, calls=%fused_computation.6 | custom fusion | bytes 384 | tf_op jit(solution)/shard_map/gather | solution.py:103
  11.1 4.6 %collective-permute-start.2 = (bf16[3,1,80,1024]{3,2,1,0:T(8,128)(2,1)S(1)}, bf16[3,1,80,1024]{3,2,1,0:T(8,128)(2,1)S(1)}, u32[]{:S(2)}, u32[]{:S(2)}) collective-permute-start(bf16[3,1,80,1024]{3,2,1,0:T(8,128)(2,1)S(1)} %constant_dynamic-update-slice_fusion), channel_id=1, source_target_pairs={{0,1},{1,2},{2,3},{3,4},{4,5},{5,6},{6,7},{8,9},{9,10},{10,11},{11... | collective-permute-start | bytes 1474568 | tf_op jit(solution)/shard_map/ppermute | solution.py:26
  15.8 1.9 %collective-permute-start.3 = (bf16[3,1,80,1024]{3,2,1,0:T(8,128)(2,1)S(1)}, bf16[3,1,80,1024]{3,2,1,0:T(8,128)(2,1)S(1)}, u32[]{:S(2)}, u32[]{:S(2)}) collective-permute-start(bf16[3,1,80,1024]{3,2,1,0:T(8,128)(2,1)S(1)} %constant_dynamic-update-slice_fusion), channel_id=1, source_target_pairs={{1,0},{2,1},{3,2},{4,3},{5,4},{6,5},{7,6},{9,8},{10,9},{11,10},{12... | collective-permute-start | bytes 1474568 | tf_op jit(solution)/shard_map/ppermute | solution.py:29
  20.1 3.9 %collective-permute-done.2 = bf16[3,1,80,1024]{3,2,1,0:T(8,128)(2,1)S(1)} collective-permute-done((bf16[3,1,80,1024]{3,2,1,0:T(8,128)(2,1)S(1)}, bf16[3,1,80,1024]{3,2,1,0:T(8,128)(2,1)S(1)}, u32[]{:S(2)}, u32[]{:S(2)}) %collective-permute-start.2) | collective-permute-done | bytes 491552 | tf_op jit(solution)/shard_map/ppermute | solution.py:26
  24.0 4.4 %collective-permute-done.3 = bf16[3,1,80,1024]{3,2,1,0:T(8,128)(2,1)S(1)} collective-permute-done((bf16[3,1,80,1024]{3,2,1,0:T(8,128)(2,1)S(1)}, bf16[3,1,80,1024]{3,2,1,0:T(8,128)(2,1)S(1)}, u32[]{:S(2)}, u32[]{:S(2)}) %collective-permute-start.3) | collective-permute-done | bytes 491552 | tf_op jit(solution)/shard_map/ppermute | solution.py:29
  29.0 1.4 %copy.96 = bf16[2,8,80,1024]{3,1,2,0:T(8,128)(2,1)S(1)} copy(bf16[2,8,80,1024]{3,2,1,0:T(8,128)(2,1)S(1)} %bitcast.304) | data formatting | bytes 5242880
  35.0 3.6 %collective-permute-start.4 = (f32[1,1,85,32]{2,3,1,0:T(8,128)S(1)}, f32[1,1,85,32]{2,3,1,0:T(8,128)S(1)}, u32[]{:S(2)}, u32[]{:S(2)}) collective-permute-start(f32[1,1,85,32]{2,3,1,0:T(8,128)S(1)} %bitcast.328), channel_id=1, source_target_pairs={{0,8},{8,16},{16,24},{1,9},{9,17},{17,25},{2,10},{10,18},{18,26},{... | collective-permute-start | bytes 32648 | tf_op jit(solution)/shard_map/ppermute | solution.py:26
  38.6 1.3 %collective-permute-start.5 = (f32[1,1,85,32]{2,3,1,0:T(8,128)S(1)}, f32[1,1,85,32]{2,3,1,0:T(8,128)S(1)}, u32[]{:S(2)}, u32[]{:S(2)}) collective-permute-start(f32[1,1,85,32]{2,3,1,0:T(8,128)S(1)} %bitcast.329), channel_id=1, source_target_pairs={{8,0},{16,8},{24,16},{9,1},{17,9},{25,17},{10,2},{18,10},{26,18},{... | collective-permute-start | bytes 32648 | tf_op jit(solution)/shard_map/ppermute | solution.py:29
  40.5 2.6 %collective-permute-done.5 = f32[1,1,85,32]{2,3,1,0:T(8,128)S(1)} collective-permute-done((f32[1,1,85,32]{2,3,1,0:T(8,128)S(1)}, f32[1,1,85,32]{2,3,1,0:T(8,128)S(1)}, u32[]{:S(2)}, u32[]{:S(2)}) %collective-permute-start.5) | collective-permute-done | bytes 10912 | tf_op jit(solution)/shard_map/ppermute | solution.py:29
  43.1 3.2 %collective-permute-start.6 = (f32[3,1,85,32]{2,3,1,0:T(8,128)S(1)}, f32[3,1,85,32]{2,3,1,0:T(8,128)S(1)}, u32[]{:S(2)}, u32[]{:S(2)}) collective-permute-start(f32[3,1,85,32]{2,3,1,0:T(8,128)S(1)} %pad_maximum_fusion.4), channel_id=1, source_target_pairs={{0,1},{1,2},{2,3},{3,4},{4,5},{5,6},{6,7},{8,9},{9,10},{10,11},{11... | collective-permute-start | bytes 97928 | tf_op jit(solution)/shard_map/ppermute | solution.py:26
  46.3 2.1 %collective-permute-start.7 = (f32[3,1,85,32]{2,3,1,0:T(8,128)S(1)}, f32[3,1,85,32]{2,3,1,0:T(8,128)S(1)}, u32[]{:S(2)}, u32[]{:S(2)}) collective-permute-start(f32[3,1,85,32]{2,3,1,0:T(8,128)S(1)} %pad_maximum_fusion.4), channel_id=1, source_target_pairs={{1,0},{2,1},{3,2},{4,3},{5,4},{6,5},{7,6},{9,8},{10,9},{11,10},{12... | collective-permute-start | bytes 97928 | tf_op jit(solution)/shard_map/ppermute | solution.py:29
  48.4 1.3 %gather_fusion.8 = f32[32]{0:T(128)} fusion(f32[64]{0:T(128)S(1)} %bitcast.295, s32[1024]{0:T(1024)S(1)} %get-tuple-element.68), kind=kCustom, calls=%fused_computation.8 | custom fusion | bytes 384 | tf_op jit(solution)/shard_map/gather | solution.py:106
  53.0 0.9 subtract_reduce_fusion.4
  54.0 0.9 subtract_reduce_fusion.5
  58.0 0.8 fusion.6
  59.6 0.8 fusion.7
  60.5 1.7 %fusion.8 = f32[12,13,8,128]{3,2,1,0:T(8,128)S(1)} fusion(f32[80,96]{0,1:T(8,128)S(1)} %bitcast.309, f32[12,8,13,128]{3,2,1,0:T(8,128)S(1)} %bitcast.314, f32[13,128]{1,0:T(8,128)} %copy-done.9, f32[80,1,128]{2,0,1:T(8,128)} %copy-done.8, f32[80,12,128]{2,0,1:T(8,128)S(1)} %bitcast.303), kind=kOutput, calls=%fused_computation.28 | convolution fusion | flops 153939968 | bytes 1847808 | tf_op jit(solution)/shard_map/dot_general | solution.py:54
  65.1 1.0 %fusion.31 = f32[1,13,128]{2,0,1:T(1,128)} fusion(f32[96,1,1]{0,1,2:T(1,128)S(1)} %reshape.1439, f32[12,13,8,128]{3,2,1,0:T(8,128)S(1)} %fusion.6), kind=kOutput, calls=%fused_computation.56 | convolution fusion | flops 1916928 | bytes 646016 | tf_op jit(solution)/shard_map/dot_general | solution.py:59
  68.6 0.8 gather_fusion.9
  70.3 3.2 %collective-permute-start.8 = (f32[1,1,85,32]{2,3,1,0:T(8,128)S(1)}, f32[1,1,85,32]{2,3,1,0:T(8,128)S(1)}, u32[]{:S(2)}, u32[]{:S(2)}) collective-permute-start(f32[1,1,85,32]{2,3,1,0:T(8,128)S(1)} %bitcast.332), channel_id=1, source_target_pairs={{0,8},{8,16},{16,24},{1,9},{9,17},{17,25},{2,10},{10,18},{18,26},{... | collective-permute-start | bytes 32648 | tf_op jit(solution)/shard_map/ppermute | solution.py:26
  73.5 1.3 %collective-permute-start.9 = (f32[1,1,85,32]{2,3,1,0:T(8,128)S(1)}, f32[1,1,85,32]{2,3,1,0:T(8,128)S(1)}, u32[]{:S(2)}, u32[]{:S(2)}) collective-permute-start(f32[1,1,85,32]{2,3,1,0:T(8,128)S(1)} %bitcast.333), channel_id=1, source_target_pairs={{8,0},{16,8},{24,16},{9,1},{17,9},{25,17},{10,2},{18,10},{26,18},{... | collective-permute-start | bytes 32648 | tf_op jit(solution)/shard_map/ppermute | solution.py:29
  74.8 3.2 %collective-permute-done.9 = f32[1,1,85,32]{2,3,1,0:T(8,128)S(1)} collective-permute-done((f32[1,1,85,32]{2,3,1,0:T(8,128)S(1)}, f32[1,1,85,32]{2,3,1,0:T(8,128)S(1)}, u32[]{:S(2)}, u32[]{:S(2)}) %collective-permute-start.9) | collective-permute-done | bytes 10912 | tf_op jit(solution)/shard_map/ppermute | solution.py:29
  78.0 5.2 %collective-permute-start.10 = (f32[3,1,85,32]{2,3,1,0:T(8,128)S(1)}, f32[3,1,85,32]{2,3,1,0:T(8,128)S(1)}, u32[]{:S(2)}, u32[]{:S(2)}) collective-permute-start(f32[3,1,85,32]{2,3,1,0:T(8,128)S(1)} %pad_maximum_fusion.5), channel_id=1, source_target_pairs={{0,1},{1,2},{2,3},{3,4},{4,5},{5,6},{6,7},{8,9},{9,10},{10,11},{11... | collective-permute-start | bytes 97928 | tf_op jit(solution)/shard_map/ppermute | solution.py:26
  83.1 2.1 %collective-permute-start.11 = (f32[3,1,85,32]{2,3,1,0:T(8,128)S(1)}, f32[3,1,85,32]{2,3,1,0:T(8,128)S(1)}, u32[]{:S(2)}, u32[]{:S(2)}) collective-permute-start(f32[3,1,85,32]{2,3,1,0:T(8,128)S(1)} %pad_maximum_fusion.5), channel_id=1, source_target_pairs={{1,0},{2,1},{3,2},{4,3},{5,4},{6,5},{7,6},{9,8},{10,9},{11,10},{12... | collective-permute-start | bytes 97928 | tf_op jit(solution)/shard_map/ppermute | solution.py:29
  85.3 4.1 %collective-permute-done.11 = f32[3,1,85,32]{2,3,1,0:T(8,128)S(1)} collective-permute-done((f32[3,1,85,32]{2,3,1,0:T(8,128)S(1)}, f32[3,1,85,32]{2,3,1,0:T(8,128)S(1)}, u32[]{:S(2)}, u32[]{:S(2)}) %collective-permute-start.11) | collective-permute-done | bytes 32672 | tf_op jit(solution)/shard_map/ppermute | solution.py:29
  92.6 0.8 fusion.9
  94.7 0.8 fusion.10
  98.5 1.4 %fusion.13 = f32[1,1,80,13,128]{4,2,3,1,0:T(8,128)} fusion(f32[80,13,128]{2,0,1:T(8,128)S(1)} %fusion.14, f32[80,13,128]{2,0,1:T(8,128)S(1)} %convolution_add_fusion.1, f32[80,96,1]{0,1,2:T(8,128)S(1)} %bitcast.326, f32[12,13,8,128]{3,2,1,0:T(8,128)S(1)} %fusion.11), kind=kOutput, calls=%fused_computation.34 | convolution fusion | flops 153620480 | bytes 2267136 | tf_op jit(solution)/shard_map/dot_general | solution.py:62
  (197 shorter events, 30.3 us)
Async XLA Ops:
  0.6 30.6 %copy-start = (bf16[1,1,4,1024,128]{4,3,2,1,0:T(8,128)(2,1)S(1)}, bf16[1,1,4,1024,128]{4,3,2,1,0:T(8,128)(2,1)}, u32[]{:S(2)}) copy-start(bf16[1,1,4,1024,128]{4,3,2,1,0:T(8,128)(2,1)} %param.11) | copy-start | bytes 3145732
  0.6 10.4 %copy-start.12 = (bf16[1,1,80,1024]{3,2,1,0:T(8,128)(2,1)S(1)}, bf16[1,1,80,1024]{3,2,1,0:T(8,128)(2,1)}, u32[]{:S(2)}) copy-start(bf16[1,1,80,1024]{3,2,1,0:T(8,128)(2,1)} %param.10) | copy-start | bytes 491524
  0.7 9.6 %copy-start.1 = (s32[1,1,64]{2,1,0:T(1,128)S(1)}, s32[1,1,64]{2,1,0:T(1,128)}, u32[]{:S(2)}) copy-start(s32[1,1,64]{2,1,0:T(1,128)} %param.16) | copy-start | bytes 772
  0.7 10.3 %copy-start.24 = (s32[1,1,4]{2,1,0:T(1,128)S(1)}, s32[1,1,4]{2,1,0:T(1,128)}, u32[]{:S(2)}) copy-start(s32[1,1,4]{2,1,0:T(1,128)} %param.12) | copy-start | bytes 52
  0.7 10.4 %collective-permute-start = (bf16[1,1,80,1024]{3,2,1,0:T(8,128)(2,1)}, bf16[1,1,80,1024]{3,2,1,0:T(8,128)(2,1)S(1)}, u32[]{:S(2)}, u32[]{:S(2)}) collective-permute-start(bf16[1,1,80,1024]{3,2,1,0:T(8,128)(2,1)} %param.10), channel_id=1, source_target_pairs={{0,8},{8,16},{16,24},{1,9},{9,17},{17,25},{2,10},{10,18},{18,26},{... | collective-permute-start | bytes 491528 | tf_op jit(solution)/shard_map/ppermute | solution.py:26
  4.0 7.1 %collective-permute-start.1 = (bf16[1,1,80,1024]{3,2,1,0:T(8,128)(2,1)}, bf16[1,1,80,1024]{3,2,1,0:T(8,128)(2,1)S(1)}, u32[]{:S(2)}, u32[]{:S(2)}) collective-permute-start(bf16[1,1,80,1024]{3,2,1,0:T(8,128)(2,1)} %param.10), channel_id=1, source_target_pairs={{8,0},{16,8},{24,16},{9,1},{17,9},{25,17},{10,2},{18,10},{26,18},{... | collective-permute-start | bytes 491528 | tf_op jit(solution)/shard_map/ppermute | solution.py:29
  6.1 11.6 %copy-start.2 = (f32[1,1,64]{2,1,0:T(1,128)S(1)}, f32[1,1,64]{2,1,0:T(1,128)}, u32[]{:S(2)}) copy-start(f32[1,1,64]{2,1,0:T(1,128)} %param.14) | copy-start | bytes 772
  7.5 11.1 %copy-start.3 = (f32[1,1,64]{2,1,0:T(1,128)S(1)}, f32[1,1,64]{2,1,0:T(1,128)}, u32[]{:S(2)}) copy-start(f32[1,1,64]{2,1,0:T(1,128)} %param.15) | copy-start | bytes 772
  11.1 12.9 %collective-permute-start.2 = (bf16[3,1,80,1024]{3,2,1,0:T(8,128)(2,1)S(1)}, bf16[3,1,80,1024]{3,2,1,0:T(8,128)(2,1)S(1)}, u32[]{:S(2)}, u32[]{:S(2)}) collective-permute-start(bf16[3,1,80,1024]{3,2,1,0:T(8,128)(2,1)S(1)} %constant_dynamic-update-slice_fusion), channel_id=1, source_target_pairs={{0,1},{1,2},{2,3},{3,4},{4,5},{5,6},{6,7},{8,9},{9,10},{10,11},{11... | collective-permute-start | bytes 1474568 | tf_op jit(solution)/shard_map/ppermute | solution.py:26
  15.8 12.7 %collective-permute-start.3 = (bf16[3,1,80,1024]{3,2,1,0:T(8,128)(2,1)S(1)}, bf16[3,1,80,1024]{3,2,1,0:T(8,128)(2,1)S(1)}, u32[]{:S(2)}, u32[]{:S(2)}) collective-permute-start(bf16[3,1,80,1024]{3,2,1,0:T(8,128)(2,1)S(1)} %constant_dynamic-update-slice_fusion), channel_id=1, source_target_pairs={{1,0},{2,1},{3,2},{4,3},{5,4},{6,5},{7,6},{9,8},{10,9},{11,10},{12... | collective-permute-start | bytes 1474568 | tf_op jit(solution)/shard_map/ppermute | solution.py:29
  31.6 28.0 %copy-start.8 = (f32[80,1,128]{2,0,1:T(8,128)}, f32[80,1,128]{2,0,1:T(8,128)S(1)}, u32[]{:S(2)}) copy-start(f32[80,1,128]{2,0,1:T(8,128)S(1)} %convolution_bitcast_fusion) | copy-start | bytes 122884
  32.1 27.5 %copy-start.9 = (f32[13,128]{1,0:T(8,128)}, f32[13,128]{1,0:T(8,128)S(1)}, u32[]{:S(2)}) copy-start(f32[13,128]{1,0:T(8,128)S(1)} %broadcast_multiply_fusion) | copy-start | bytes 19972
  35.0 5.5 %collective-permute-start.4 = (f32[1,1,85,32]{2,3,1,0:T(8,128)S(1)}, f32[1,1,85,32]{2,3,1,0:T(8,128)S(1)}, u32[]{:S(2)}, u32[]{:S(2)}) collective-permute-start(f32[1,1,85,32]{2,3,1,0:T(8,128)S(1)} %bitcast.328), channel_id=1, source_target_pairs={{0,8},{8,16},{16,24},{1,9},{9,17},{17,25},{2,10},{10,18},{18,26},{... | collective-permute-start | bytes 32648 | tf_op jit(solution)/shard_map/ppermute | solution.py:26
  38.6 4.5 %collective-permute-start.5 = (f32[1,1,85,32]{2,3,1,0:T(8,128)S(1)}, f32[1,1,85,32]{2,3,1,0:T(8,128)S(1)}, u32[]{:S(2)}, u32[]{:S(2)}) collective-permute-start(f32[1,1,85,32]{2,3,1,0:T(8,128)S(1)} %bitcast.329), channel_id=1, source_target_pairs={{8,0},{16,8},{24,16},{9,1},{17,9},{25,17},{10,2},{18,10},{26,18},{... | collective-permute-start | bytes 32648 | tf_op jit(solution)/shard_map/ppermute | solution.py:29
  43.1 8.7 %collective-permute-start.6 = (f32[3,1,85,32]{2,3,1,0:T(8,128)S(1)}, f32[3,1,85,32]{2,3,1,0:T(8,128)S(1)}, u32[]{:S(2)}, u32[]{:S(2)}) collective-permute-start(f32[3,1,85,32]{2,3,1,0:T(8,128)S(1)} %pad_maximum_fusion.4), channel_id=1, source_target_pairs={{0,1},{1,2},{2,3},{3,4},{4,5},{5,6},{6,7},{8,9},{9,10},{10,11},{11... | collective-permute-start | bytes 97928 | tf_op jit(solution)/shard_map/ppermute | solution.py:26
  46.3 6.3 %collective-permute-start.7 = (f32[3,1,85,32]{2,3,1,0:T(8,128)S(1)}, f32[3,1,85,32]{2,3,1,0:T(8,128)S(1)}, u32[]{:S(2)}, u32[]{:S(2)}) collective-permute-start(f32[3,1,85,32]{2,3,1,0:T(8,128)S(1)} %pad_maximum_fusion.4), channel_id=1, source_target_pairs={{1,0},{2,1},{3,2},{4,3},{5,4},{6,5},{7,6},{9,8},{10,9},{11,10},{12... | collective-permute-start | bytes 97928 | tf_op jit(solution)/shard_map/ppermute | solution.py:29
  48.4 9.3 %copy-start.20 = (f32[128]{0:T(128)}, f32[128]{0:T(128)S(1)}, u32[]{:S(2)}) copy-start(f32[128]{0:T(128)S(1)} %get-tuple-element.70) | copy-start | bytes 1540
  48.4 9.3 %copy-start.22 = (f32[128]{0:T(128)}, f32[128]{0:T(128)S(1)}, u32[]{:S(2)}) copy-start(f32[128]{0:T(128)S(1)} %get-tuple-element.71) | copy-start | bytes 1540
  60.5 2.4 %copy-start.7 = (f32[80,13,128]{2,0,1:T(8,128)S(1)}, f32[80,13,128]{2,0,1:T(8,128)}, u32[]{:S(2)}) copy-start(f32[80,13,128]{2,0,1:T(8,128)} %copy-done.6) | copy-start | bytes 1597444
  60.5 2.4 %copy-start.11 = (f32[80,3,32]{0,2,1:T(8,128)S(1)}, f32[80,3,32]{0,2,1:T(8,128)}, u32[]{:S(2)}) copy-start(f32[80,3,32]{0,2,1:T(8,128)} %bitcast_multiply_fusion.7) | copy-start | bytes 92164
  62.9 3.2 %copy-start.19 = (f32[3,32]{1,0:T(4,128)S(1)}, f32[3,32]{1,0:T(4,128)}, u32[]{:S(2)}) copy-start(f32[3,32]{1,0:T(4,128)} %get-tuple-element.31) | copy-start | bytes 1156
  63.5 3.6 %copy-start.14 = (f32[13,128]{1,0:T(8,128)S(1)}, f32[13,128]{1,0:T(8,128)}, u32[]{:S(2)}) copy-start(f32[13,128]{1,0:T(8,128)} %copy-done.13) | copy-start | bytes 19972
  64.3 5.9 %copy-start.15 = (f32[1,32]{0,1:T(8,128)S(1)}, f32[1,32]{0,1:T(8,128)}, u32[]{:S(2)}) copy-start(f32[1,32]{0,1:T(8,128)} %get-tuple-element.44) | copy-start | bytes 388
  64.3 5.9 %copy-start.16 = (f32[1,32]{0,1:T(8,128)S(1)}, f32[1,32]{0,1:T(8,128)}, u32[]{:S(2)}) copy-start(f32[1,32]{0,1:T(8,128)} %get-tuple-element.45) | copy-start | bytes 388
  66.1 4.1 %copy-start.17 = (f32[1,32]{0,1:T(8,128)S(1)}, f32[1,32]{0,1:T(8,128)}, u32[]{:S(2)}) copy-start(f32[1,32]{0,1:T(8,128)} %copy.62) | copy-start | bytes 388
  66.1 4.1 %copy-start.18 = (f32[1,32]{0,1:T(8,128)S(1)}, f32[1,32]{0,1:T(8,128)}, u32[]{:S(2)}) copy-start(f32[1,32]{0,1:T(8,128)} %copy.61) | copy-start | bytes 388
  67.8 24.5 %copy-start.21 = (f32[128]{0:T(128)S(1)}, f32[128]{0:T(128)}, u32[]{:S(2)}) copy-start(f32[128]{0:T(128)} %copy-done.20) | copy-start | bytes 1540
  67.8 24.5 %copy-start.23 = (f32[128]{0:T(128)S(1)}, f32[128]{0:T(128)}, u32[]{:S(2)}) copy-start(f32[128]{0:T(128)} %copy-done.22) | copy-start | bytes 1540
  70.3 4.5 %collective-permute-start.8 = (f32[1,1,85,32]{2,3,1,0:T(8,128)S(1)}, f32[1,1,85,32]{2,3,1,0:T(8,128)S(1)}, u32[]{:S(2)}, u32[]{:S(2)}) collective-permute-start(f32[1,1,85,32]{2,3,1,0:T(8,128)S(1)} %bitcast.332), channel_id=1, source_target_pairs={{0,8},{8,16},{16,24},{1,9},{9,17},{17,25},{2,10},{10,18},{18,26},{... | collective-permute-start | bytes 32648 | tf_op jit(solution)/shard_map/ppermute | solution.py:26
  73.5 4.5 %collective-permute-start.9 = (f32[1,1,85,32]{2,3,1,0:T(8,128)S(1)}, f32[1,1,85,32]{2,3,1,0:T(8,128)S(1)}, u32[]{:S(2)}, u32[]{:S(2)}) collective-permute-start(f32[1,1,85,32]{2,3,1,0:T(8,128)S(1)} %bitcast.333), channel_id=1, source_target_pairs={{8,0},{16,8},{24,16},{9,1},{17,9},{25,17},{10,2},{18,10},{26,18},{... | collective-permute-start | bytes 32648 | tf_op jit(solution)/shard_map/ppermute | solution.py:29
  78.0 7.3 %collective-permute-start.10 = (f32[3,1,85,32]{2,3,1,0:T(8,128)S(1)}, f32[3,1,85,32]{2,3,1,0:T(8,128)S(1)}, u32[]{:S(2)}, u32[]{:S(2)}) collective-permute-start(f32[3,1,85,32]{2,3,1,0:T(8,128)S(1)} %pad_maximum_fusion.5), channel_id=1, source_target_pairs={{0,1},{1,2},{2,3},{3,4},{4,5},{5,6},{6,7},{8,9},{9,10},{10,11},{11... | collective-permute-start | bytes 97928 | tf_op jit(solution)/shard_map/ppermute | solution.py:26
  83.1 6.3 %collective-permute-start.11 = (f32[3,1,85,32]{2,3,1,0:T(8,128)S(1)}, f32[3,1,85,32]{2,3,1,0:T(8,128)S(1)}, u32[]{:S(2)}, u32[]{:S(2)}) collective-permute-start(f32[3,1,85,32]{2,3,1,0:T(8,128)S(1)} %pad_maximum_fusion.5), channel_id=1, source_target_pairs={{1,0},{2,1},{3,2},{4,3},{5,4},{6,5},{7,6},{9,8},{10,9},{11,10},{12... | collective-permute-start | bytes 97928 | tf_op jit(solution)/shard_map/ppermute | solution.py:29
  (5 other events, 6.0 us)
where the time goes:
time: 101 us; the launch traced here: 100 us
  starting transfers between devices  33.1 us (33%)
  local copies, waits for them, and re-layouts  22.4 us (22%)
  waiting for transfers between devices  19 us (19%)
  matrix products  14.5 us (14%)
  other arithmetic  9.46 us (9%)
  between operations  1.53 us (2%)
    ppermute x6, starting transfers between devices, extended(): lax.ppermute(lax.slice_in_dim(block, block.shape[dim] - width, None, axis...  23.1 us
    ppermute x6, waiting for transfers between devices, extended(): lax.ppermute(lax.slice_in_dim(block, 0, width, axis=dim), axis, backward)  15.1 us
    ppermute x6, starting transfers between devices, extended(): lax.ppermute(lax.slice_in_dim(block, 0, width, axis=dim), axis, backward)  10 us
    dot_general x6, matrix products, update_group(): jnp.dot(observed.T, flat_anomaly, precision=exact_mode, preferred_element...  5.78 us
    dot_general x6, matrix products, update_group(): jnp.dot(observed * damping[None, :], gain, precision=exact_mode, preferre...  4.66 us
    ppermute x6, waiting for transfers between devices, extended(): lax.ppermute(lax.slice_in_dim(block, block.shape[dim] - width, None, axis...  3.91 us
    unnamed x55, local copies, waits for them, and re-layouts  3.87 us
    dot_general x6, matrix products, update_group(): jnp.dot(innovation[None, :], gain, precision=exact_mode, preferred_elemen...  3.1 us
  transfers between devices with their start and end apart: 12, of which 6 were waited for; matrix products, arithmetic and copies ran while one was open for 12% of the time, Pallas kernels for 0%

commit v1 on v0

v1 whole, which is shorter than its diff:
```python
import functools

import jax
import jax.numpy as jnp
import numpy as np
from jax import lax
from jax.experimental import pallas as pl
from jax.experimental.pallas import tpu as pltpu
from jax.sharding import PartitionSpec as P

AX = 8
AY = 16
OB = 32
NB = 2
RAD = 2
CODE = 64

MESH = pl.DeviceIdType.MESH
OFFS = [(dx, dy) for dx in (-1, 0, 1) for dy in (-1, 0, 1)]
OTHERS = [i for i in range(9) if i != 4]


def taper_of(dx, dy):
    return max(1.0 - (dx * dx + dy * dy) / float(RAD * RAD), 0.0) ** 2


@functools.lru_cache
def tables():
    cells = AX * AY
    own = [(c // AY, c % AY) for c in range(cells)]
    halo = [
        (x, y)
        for x in range(-RAD, AX + RAD)
        for y in range(-RAD, AY + RAD)
        if not (0 <= x < AX and 0 <= y < AY)
    ]
    lanes = own + halo
    where = {xy: n for n, xy in enumerate(lanes)}
    code = np.full((8, 2 * cells), -1.0, np.float32)
    for n, (x, y) in enumerate(lanes):
        code[:, n] = (x + AX) * CODE + (y + AY)
    move = np.zeros((2 * cells, 2, 8, cells), np.float32)
    for n, (x, y) in enumerate(lanes):
        for d, i in enumerate(OTHERS):
            dx, dy = OFFS[i]
            src = where.get((x + dx, y + dy))
            if src is not None:
                move[src, n // cells, d, n % cells] = 1.0
    pick = np.zeros((8, cells, cells), np.float32)
    for n, (x, y) in enumerate(halo):
        i = (x // AX + 1) * 3 + (y // AY + 1)
        pick[OTHERS.index(i), (x % AX) * AY + (y % AY), n] = 1.0
    return code, move.reshape(2 * cells, 16 * cells), pick.reshape(8 * cells, cells)


def exchange_kernel(
    src_ref, meta_ref, ocean_ref, weights_ref, atm_ref,
    tiles_ref, metat_ref, fields_ref, fmean_ref,
    ocn, wts, meta, local_sem, send_sem, recv_sem,
):
    gx, gy = lax.axis_index("gx"), lax.axis_index("gy")
    nx, ny = lax.axis_size("gx"), lax.axis_size("gy")
    members = tiles_ref.shape[1]
    fields = fields_ref.shape[0]

    def there(i):
        dx, dy = OFFS[i]
        return (gx + dx >= 0) & (gx + dx < nx) & (gy + dy >= 0) & (gy + dy < ny)

    own_in = pltpu.make_async_copy(ocean_ref, ocn.at[4], local_sem.at[0])
    own_in.start()
    w_in = pltpu.make_async_copy(weights_ref, wts, local_sem.at[1])
    w_in.start()
    atm_in = pltpu.make_async_copy(atm_ref, fields_ref, local_sem.at[2])
    atm_in.start()

    barrier = pltpu.get_barrier_semaphore()
    for i in OTHERS:
        dx, dy = OFFS[i]

        @pl.when(there(i))
        def _():
            pl.semaphore_signal(barrier, inc=1, device_id=(gx + dx, gy + dy), device_id_type=MESH)

    rows = meta_ref[...]
    order = rows[0:1, :]
    slot = lax.broadcasted_iota(jnp.int32, (rows.shape[1], rows.shape[1]), 0).astype(jnp.float32)
    perm = jnp.where(order == slot, 1.0, 0.0)
    meta[4] = jnp.dot(
        rows, perm, precision=lax.Precision.HIGHEST, preferred_element_type=jnp.float32
    )
    for n in range(9, meta.shape[0]):
        meta[n] = jnp.zeros(meta.shape[1:], jnp.float32)
    across = 1 + (gx > 0).astype(jnp.int32) + (gx < nx - 1).astype(jnp.int32)
    along = 1 + (gy > 0).astype(jnp.int32) + (gy < ny - 1).astype(jnp.int32)
    pl.semaphore_wait(barrier, across * along - 1)
    for i in OTHERS:

        @pl.when(jnp.logical_not(there(i)))
        def _():
            tiles_ref[i] = jnp.zeros(tiles_ref.shape[1:], jnp.float32)
            meta[i] = jnp.zeros(meta.shape[1:], jnp.float32)

    own_in.wait()

    def remote(buf, kind, i):
        dx, dy = OFFS[i]
        return pltpu.make_async_remote_copy(
            src_ref=buf.at[4],
            dst_ref=buf.at[8 - i],
            send_sem=send_sem.at[kind, i],
            recv_sem=recv_sem.at[kind, 8 - i],
            device_id=(gx + dx, gy + dy),
            device_id_type=MESH,
        )

    def arrival(buf, kind, i):
        return pltpu.make_async_remote_copy(
            src_ref=buf.at[4],
            dst_ref=buf.at[i],
            send_sem=send_sem.at[kind, i],
            recv_sem=recv_sem.at[kind, i],
            device_id=(gx + OFFS[i][0], gy + OFFS[i][1]),
            device_id_type=MESH,
        )

    def send(buf, kind):
        for i in OTHERS:

            @pl.when(there(i))
            def _():
                remote(buf, kind, i).start()

    def receive(buf, kind):
        for i in OTHERS:

            @pl.when(there(i))
            def _():
                arrival(buf, kind, i).wait_recv()

    def settle(buf, kind):
        for i in OTHERS:

            @pl.when(there(i))
            def _():
                remote(buf, kind, i).wait_send()

    send(ocn, 0)
    send(meta, 1)

    atm_in.wait()
    for v in range(fields):
        block = fields_ref[v]
        mean = jnp.sum(block, axis=0, keepdims=True) / members
        fmean_ref[v : v + 1, :] = mean
        fields_ref[v] = block - mean
    receive(meta, 1)
    flat = meta[...].reshape(meta.shape[0] * meta.shape[1], meta.shape[2])
    metat_ref[...] = flat.T
    w_in.wait()
    receive(ocn, 0)
    total = jnp.zeros(tiles_ref.shape[1:], jnp.float32)
    for k in range(wts.shape[0]):
        source = src_ref[k]
        position = (source // ny - gx + 1) * 3 + (source % ny - gy + 1)
        position = jnp.clip(position, 0, 8)
        total += jnp.dot(ocn[position], wts[k], preferred_element_type=jnp.float32)
    tiles_ref[4] = total
    send(tiles_ref, 2)
    settle(ocn, 0)
    settle(meta, 1)
    receive(tiles_ref, 2)
    settle(tiles_ref, 2)


def split_rows(block):
    high = block.astype(jnp.bfloat16).astype(jnp.float32)
    return jnp.concatenate([high, block - high], axis=0).astype(jnp.bfloat16)


def analysis_kernel(
    tiles_ref, metat_ref, fields_ref, fmean_ref, code_ref, move_ref, pick_ref,
    mean_ref, anom_ref,
    held, shifted, out_sem,
):
    fields, members, cells = fields_ref.shape
    scale = 1.0 / (members - 1)
    beside = split_rows(jnp.concatenate([tiles_ref[i] for i in OTHERS], axis=1))
    halo = jnp.dot(beside, pick_ref[...], preferred_element_type=jnp.float32)
    grid = jnp.concatenate([tiles_ref[4], halo[:members] + halo[members:]], axis=1)
    gmean = jnp.sum(grid, axis=0, keepdims=True) / members
    grid = grid - gmean
    code = code_ref[0:1, :]

    for b in range(NB):
        last = b == NB - 1
        variance = jnp.sum(grid * grid, axis=0, keepdims=True) / (members - 1)
        gains = jnp.zeros((OB, 2 * cells), jnp.float32)
        sums = jnp.zeros((OB, 2 * cells), jnp.float32)
        weights = jnp.zeros((OB, 2 * cells), jnp.float32)
        for i in range(9):
            dx, dy = OFFS[i]
            column = metat_ref[b * OB : (b + 1) * OB, 8 * i : 8 * i + 8]
            spot = column[:, 1:2] + float((AX * dx + AX) * CODE + AY * dy + AY)
            error = column[:, 3:4]
            live = column[:, 4:5]
            denom = variance + (error + (1.0 - live))
            weighting = live / denom
            damping = 1.0 / (1.0 + jnp.sqrt(error / denom))
            hit = spot == code
            weighting = jnp.where(hit, weighting, 0.0)
            weights = weights + weighting
            gains = gains + weighting * damping
            sums = sums + weighting * column[:, 2:3]
        alpha = jnp.sum(gains, axis=0, keepdims=True)
        beta = jnp.sum(sums, axis=0, keepdims=True) - gmean * jnp.sum(weights, axis=0, keepdims=True)
        extra = jnp.concatenate([alpha, beta, jnp.zeros((6, 2 * cells), jnp.float32)], axis=0)
        left = split_rows(jnp.concatenate([grid, extra], axis=0))
        width = (8 if last else 16) * cells
        moved = jnp.dot(left, move_ref[:, :width], preferred_element_type=jnp.float32)
        rows = members + 8
        shifted[:, :width] = moved[:rows] + moved[rows:]

        def step(block, part, center, alpha, beta):
            total = jnp.zeros_like(block)
            mean = jnp.zeros((1, cells), jnp.float32)
            for d in range(9):
                if d == 8:
                    source, a, m = center, alpha * scale, beta * scale
                else:
                    dx, dy = OFFS[OTHERS[d]]
                    weight = scale * taper_of(dx, dy)
                    at = (part * 8 + d) * cells
                    source = shifted[:members, at : at + cells]
                    a = shifted[members : members + 1, at : at + cells] * weight
                    m = shifted[members + 1 : members + 2, at : at + cells] * weight
                cov = jnp.sum(block * source, axis=0, keepdims=True)
                mean = mean + cov * m
                total = total + source * (cov * a)
            return block - total, mean

        own = grid[:, :cells]
        held[fields] = own
        own_args = (alpha[:, :cells], beta[:, :cells])
        origin = fields_ref if b == 0 else held

        def one_field(v, carry, origin=origin, own_args=own_args, last=last, b=b, step=step):
            block, mean = step(origin[v], 0, held[fields], *own_args)
            held[v] = block
            before = fmean_ref[pl.ds(v, 1), :] if b == 0 else mean_ref[pl.ds(v, 1), :]
            mean_ref[pl.ds(v, 1), :] = before + mean
            if last:
                pltpu.make_async_copy(held.at[v], anom_ref.at[v], out_sem.at[v]).start()
            return carry

        lax.fori_loop(0, fields, one_field, 0)
        block, mean = step(own, 0, own, *own_args)
        if last:
            held[fields] = block
            mean_ref[fields : fields + 1, :] = gmean[:, :cells] + mean
            pltpu.make_async_copy(
                held.at[fields], anom_ref.at[fields], out_sem.at[fields]
            ).start()
            for v in range(fields + 1):
                pltpu.make_async_copy(held.at[v], anom_ref.at[v], out_sem.at[v]).wait()
        else:
            outer = grid[:, cells:]
            far, far_mean = step(outer, 1, outer, alpha[:, cells:], beta[:, cells:])
            grid = jnp.concatenate([block, far], axis=1)
            gmean = gmean + jnp.concatenate([mean, far_mean], axis=1)


def local(
    atm_members, ocean_members, remap_weights, pair_src, obs_cell, obs_value, obs_error,
    obs_live, obs_order,
):
    members, fields, cells = atm_members.shape[2:]
    slots = obs_cell.shape[2]
    sources, depth = remap_weights.shape[2:4]
    cell = obs_cell[0, 0]
    spot = ((cell // AY) * CODE + cell % AY).astype(jnp.float32)
    meta = jnp.stack(
        [
            obs_order[0, 0].astype(jnp.float32), spot, obs_value[0, 0], obs_error[0, 0],
            obs_live[0, 0].astype(jnp.float32),
        ]
    )
    meta = jnp.pad(meta, ((0, 3), (0, cells - slots)))
    vmem = pl.BlockSpec(memory_space=pltpu.VMEM)
    hbm = pl.BlockSpec(memory_space=pltpu.HBM)
    tiles, metat, anomalies, fmean = pl.pallas_call(
        exchange_kernel,
        out_shape=(
            jax.ShapeDtypeStruct((9, members, cells), jnp.float32),
            jax.ShapeDtypeStruct((128, 128), jnp.float32),
            jax.ShapeDtypeStruct((fields, members, cells), jnp.float32),
            jax.ShapeDtypeStruct((fields, cells), jnp.float32),
        ),
        in_specs=[pl.BlockSpec(memory_space=pltpu.SMEM), vmem, hbm, hbm, hbm],
        out_specs=(vmem,) * 4,
        scratch_shapes=[
            pltpu.VMEM((9, members, depth), jnp.bfloat16),
            pltpu.VMEM((sources, depth, cells), jnp.bfloat16),
            pltpu.VMEM((16, 8, 128), jnp.float32),
            pltpu.SemaphoreType.DMA((3,)),
            pltpu.SemaphoreType.DMA((3, 9)),
            pltpu.SemaphoreType.DMA((3, 9)),
        ],
        compiler_params=pltpu.CompilerParams(
            collective_id=0, has_side_effects=True, vmem_limit_bytes=16 << 20
        ),
        name="exchange",
    )(pair_src[0, 0], meta, ocean_members[0, 0], remap_weights[0, 0],
        jnp.transpose(atm_members[0, 0], (1, 0, 2)))
    code, move, pick = tables()
    post_mean, post_anom = pl.pallas_call(
        analysis_kernel,
        out_shape=(
            jax.ShapeDtypeStruct((fields + 1, cells), jnp.float32),
            jax.ShapeDtypeStruct((fields + 1, members, cells), jnp.float32),
        ),
        in_specs=[vmem] * 7,
        out_specs=(vmem, hbm),
        scratch_shapes=[
            pltpu.VMEM((fields + 1, members, cells), jnp.float32),
            pltpu.VMEM((members + 8, 16 * cells), jnp.float32),
            pltpu.SemaphoreType.DMA((fields + 1,)),
        ],
        compiler_params=pltpu.CompilerParams(vmem_limit_bytes=24 << 20),
        name="analysis",
    )(
        tiles, metat, anomalies, fmean, jnp.asarray(code),
        jnp.asarray(move, jnp.bfloat16), jnp.asarray(pick, jnp.bfloat16),
    )
    return (post_mean[None, None], jnp.transpose(post_anom, (1, 0, 2))[None, None])


def solution(mesh):
    in_specs = (
        P("gx", "gy", None, None, None),
        P("gx", "gy", None, None),
        P("gx", "gy", None, None, None),
        P("gx", "gy", None),
        P("gx", "gy", None),
        P("gx", "gy", None),
        P("gx", "gy", None),
        P("gx", "gy", None),
        P("gx", "gy", None),
    )
    out_specs = (P("gx", "gy", None, None), P("gx", "gy", None, None, None))
    return jax.shard_map(local, mesh=mesh, in_specs=in_specs, out_specs=out_specs, check_vma=False)
```

time: 101 us -> 35.5 us (0.35)
  the two profiles are of different devices: /device:TPU:3 before, /device:TPU:4 now
where the time goes in v1:
time: 35.5 us; the launch traced here: 35.2 us
  Pallas kernels  28.1 us (79%)
  local copies, waits for them, and re-layouts  6.42 us (18%)
  between operations  0.7 us (2%)
    pallas_call x1, Pallas kernels, local(): pl.pallas_call(exchange_kernel, out_shape=(jax.ShapeDtypeStruct((9, membe...  24.2 us
    unnamed x25, local copies, waits for them, and re-layouts  6.39 us
    pallas_call x1, Pallas kernels, local(): pl.pallas_call(analysis_kernel, out_shape=(jax.ShapeDtypeStruct((fields +...  3.89 us

profile of v1, /device:TPU:4, one launch (start us, length us, event | category | flops | bytes accessed | tf_op | source)
XLA Modules:
  0.0 35.2 jit_solution(516410332201630107)
XLA Ops:
  0.6 0.0 copy-start.11
  0.6 0.6 %copy-done.11 = s32[1,1,64]{2,1,0:T(1,128)S(1)} copy-done((s32[1,1,64]{2,1,0:T(1,128)S(1)}, s32[1,1,64]{2,1,0:T(1,128)}, u32[]{:S(2)}) %copy-start.11) | copy-done | bytes 280
  1.3 0.0 copy-start.7
  1.3 0.0 copy-start.8
  1.3 0.6 %copy-done.7 = s32[1,1,64]{2,1,0:T(1,128)S(1)} copy-done((s32[1,1,64]{2,1,0:T(1,128)S(1)}, s32[1,1,64]{2,1,0:T(1,128)}, u32[]{:S(2)}) %copy-start.7) | copy-done | bytes 280
  1.9 0.0 copy-done.8
  2.0 0.0 copy-start.9
  2.0 0.0 copy-start.10
  2.0 0.7 %copy-done.9 = f32[1,1,64]{2,1,0:T(1,128)S(1)} copy-done((f32[1,1,64]{2,1,0:T(1,128)S(1)}, f32[1,1,64]{2,1,0:T(1,128)}, u32[]{:S(2)}) %copy-start.9) | copy-done | bytes 280
  2.6 0.0 copy-done.10
  2.7 0.0 copy-start.6
  2.7 0.6 %copy-done.6 = s32[1,1,4]{2,1,0:T(1,128)S(1)} copy-done((s32[1,1,4]{2,1,0:T(1,128)S(1)}, s32[1,1,4]{2,1,0:T(1,128)}, u32[]{:S(2)}) %copy-start.6) | copy-done | bytes 40
  3.3 0.0 copy-start
  3.3 1.2 %copy-done = bf16[1,1,4,1024,128]{4,3,2,1,0:T(8,128)(2,1)S(1)} copy-done((bf16[1,1,4,1024,128]{4,3,2,1,0:T(8,128)(2,1)S(1)}, bf16[1,1,4,1024,128]{4,3,2,1,0:T(8,128)(2,1)}, u32[]{:S(2)}) %copy-start) | copy-done | bytes 1048600
  4.5 0.0 copy-start.2
  4.5 1.0 %copy-done.2 = f32[1,1,80,12,128]{4,2,3,1,0:T(8,128)S(1)} copy-done((f32[1,1,80,12,128]{4,2,3,1,0:T(8,128)S(1)}, f32[1,1,80,12,128]{4,2,3,1,0:T(8,128)}, u32[]{:S(2)}) %copy-start.2) | copy-done | bytes 491544
  5.6 0.0 copy-start.4
  5.6 0.9 %copy-done.4 = bf16[1,1,80,1024]{3,2,1,0:T(8,128)(2,1)S(1)} copy-done((bf16[1,1,80,1024]{3,2,1,0:T(8,128)(2,1)S(1)}, bf16[1,1,80,1024]{3,2,1,0:T(8,128)(2,1)}, u32[]{:S(2)}) %copy-start.4) | copy-done | bytes 163864
  6.5 0.0 copy-start.1
  6.5 0.0 copy-start.3
  6.5 0.0 copy-start.5
  6.5 24.2 %exchange.1 = (f32[9,80,128]{2,1,0:T(8,128)S(1)}, f32[128,128]{1,0:T(8,128)S(1)}, f32[12,80,128]{2,1,0:T(8,128)S(1)}, f32[12,128]{1,0:T(8,128)S(1)}) custom-call(s32[4]{0:T(128)S(1)} %bitcast.35, f32[8,128]{1,0:T(8,128)S(1)} %pad.4.meta_ref, bf16[80,1024]{1,0:T(8,128)(2,1)S(1)} %bitcast.33, bf16[4,1024,128]{2,1,0:T(8,128)(2,1)S(1)} %bitcast.31, ...), custom_call_target="tpu_custom_call" | custom-call | tf_op jit(solution)/shard_map/exchange/pallas_call | solution.py:291
  30.7 0.0 copy-done.1
  30.7 0.0 copy-done.3
  30.7 0.0 copy-done.5
  30.7 3.9 %analysis.1 = (f32[13,128]{1,0:T(8,128)S(1)}, f32[13,80,128]{2,1,0:T(8,128)}) custom-call(f32[9,80,128]{2,1,0:T(8,128)S(1)} %get-tuple-element.8.tiles_ref, f32[128,128]{1,0:T(8,128)S(1)} %get-tuple-element.9.metat_ref, f32[12,80,128]{2,1,0:T(8,128)S(1)} %get-tuple-element.10.fields_ref, f32[12,128]{1,0:T(8,128)S(1)} %get-tuple-element.11.fmean_ref, ...), custom_call_target="tpu_custom_call" | custom-call | tf_op jit(solution)/shard_map/analysis/pallas_call | solution.py:316
  34.6 0.6 %copy.14 = f32[1,1,13,128]{3,1,2,0:T(1,128)} copy(f32[1,1,13,128]{3,2,1,0:T(8,128)S(1)} %bitcast.34) | data formatting | bytes 13312
  (4 shorter events, 0.0 us)
Async XLA Ops:
  0.6 0.7 %copy-start.11 = (s32[1,1,64]{2,1,0:T(1,128)S(1)}, s32[1,1,64]{2,1,0:T(1,128)}, u32[]{:S(2)}) copy-start(s32[1,1,64]{2,1,0:T(1,128)} %param.16) | copy-start | bytes 772
  1.3 0.7 %copy-start.7 = (s32[1,1,64]{2,1,0:T(1,128)S(1)}, s32[1,1,64]{2,1,0:T(1,128)}, u32[]{:S(2)}) copy-start(s32[1,1,64]{2,1,0:T(1,128)} %param.19) | copy-start | bytes 772
  1.3 0.7 %copy-start.8 = (s32[1,1,64]{2,1,0:T(1,128)S(1)}, s32[1,1,64]{2,1,0:T(1,128)}, u32[]{:S(2)}) copy-start(s32[1,1,64]{2,1,0:T(1,128)} %param.20) | copy-start | bytes 772
  2.0 0.7 %copy-start.9 = (f32[1,1,64]{2,1,0:T(1,128)S(1)}, f32[1,1,64]{2,1,0:T(1,128)}, u32[]{:S(2)}) copy-start(f32[1,1,64]{2,1,0:T(1,128)} %param.17) | copy-start | bytes 772
  2.0 0.7 %copy-start.10 = (f32[1,1,64]{2,1,0:T(1,128)S(1)}, f32[1,1,64]{2,1,0:T(1,128)}, u32[]{:S(2)}) copy-start(f32[1,1,64]{2,1,0:T(1,128)} %param.18) | copy-start | bytes 772
  2.7 0.7 %copy-start.6 = (s32[1,1,4]{2,1,0:T(1,128)S(1)}, s32[1,1,4]{2,1,0:T(1,128)}, u32[]{:S(2)}) copy-start(s32[1,1,4]{2,1,0:T(1,128)} %param.15) | copy-start | bytes 52
  3.3 1.2 %copy-start = (bf16[1,1,4,1024,128]{4,3,2,1,0:T(8,128)(2,1)S(1)}, bf16[1,1,4,1024,128]{4,3,2,1,0:T(8,128)(2,1)}, u32[]{:S(2)}) copy-start(bf16[1,1,4,1024,128]{4,3,2,1,0:T(8,128)(2,1)} %param.14) | copy-start | bytes 3145732
  4.5 1.0 %copy-start.2 = (f32[1,1,80,12,128]{4,2,3,1,0:T(8,128)S(1)}, f32[1,1,80,12,128]{4,2,3,1,0:T(8,128)}, u32[]{:S(2)}) copy-start(f32[1,1,80,12,128]{4,2,3,1,0:T(8,128)} %param.12) | copy-start | bytes 1474564
  5.6 0.9 %copy-start.4 = (bf16[1,1,80,1024]{3,2,1,0:T(8,128)(2,1)S(1)}, bf16[1,1,80,1024]{3,2,1,0:T(8,128)(2,1)}, u32[]{:S(2)}) copy-start(bf16[1,1,80,1024]{3,2,1,0:T(8,128)(2,1)} %param.13) | copy-start | bytes 491524
  6.5 24.2 %copy-start.1 = (bf16[256,2048]{1,0:T(8,128)(2,1)S(1)}, bf16[256,2048]{1,0:T(8,128)(2,1)}, u32[]{:S(2)}) copy-start(bf16[256,2048]{1,0:T(8,128)(2,1)} %constant.40.clone.move_ref) | copy-start | bytes 3145732
  6.5 24.2 %copy-start.3 = (bf16[1024,128]{1,0:T(8,128)(2,1)S(1)}, bf16[1024,128]{1,0:T(8,128)(2,1)}, u32[]{:S(2)}) copy-start(bf16[1024,128]{1,0:T(8,128)(2,1)} %constant.41.clone.pick_ref) | copy-start | bytes 786436
  6.5 24.2 %copy-start.5 = (f32[8,256]{1,0:T(8,128)S(1)}, f32[8,256]{1,0:T(8,128)}, u32[]{:S(2)}) copy-start(f32[8,256]{1,0:T(8,128)} %constant.39.clone.code_ref) | copy-start | bytes 24580

commit v2 on v1

v2 whole, which is shorter than its diff:
```python
import functools

import jax
import jax.numpy as jnp
import numpy as np
from jax import lax
from jax.experimental import pallas as pl
from jax.experimental.pallas import tpu as pltpu
from jax.sharding import PartitionSpec as P

AX = 8
AY = 16
OB = 32
NB = 2
RAD = 2
CODE = 64
LIMIT = 66977792

MESH = pl.DeviceIdType.MESH
OFFS = [(dx, dy) for dx in (-1, 0, 1) for dy in (-1, 0, 1)]
OTHERS = [i for i in range(9) if i != 4]


def taper_of(dx, dy):
    return max(1.0 - (dx * dx + dy * dy) / float(RAD * RAD), 0.0) ** 2


@functools.lru_cache
def tables():
    cells = AX * AY
    own = [(c // AY, c % AY) for c in range(cells)]
    halo = [
        (x, y)
        for x in range(-RAD, AX + RAD)
        for y in range(-RAD, AY + RAD)
        if not (0 <= x < AX and 0 <= y < AY)
    ]
    lanes = own + halo
    where = {xy: n for n, xy in enumerate(lanes)}
    code = np.full((8, 2 * cells), -1.0, np.float32)
    for n, (x, y) in enumerate(lanes):
        code[:, n] = (x + AX) * CODE + (y + AY)
    move = np.zeros((2 * cells, 2, 8, cells), np.float32)
    for n, (x, y) in enumerate(lanes):
        for d, i in enumerate(OTHERS):
            dx, dy = OFFS[i]
            src = where.get((x + dx, y + dy))
            if src is not None:
                move[src, n // cells, d, n % cells] = 1.0
    pick = np.zeros((8, cells, cells), np.float32)
    for n, (x, y) in enumerate(halo):
        i = (x // AX + 1) * 3 + (y // AY + 1)
        pick[OTHERS.index(i), (x % AX) * AY + (y % AY), n] = 1.0
    return code, move.reshape(2 * cells, 16 * cells), pick.reshape(8 * cells, cells)


def split_rows(block):
    high = block.astype(jnp.bfloat16).astype(jnp.float32)
    return jnp.concatenate([high, block - high], axis=0).astype(jnp.bfloat16)


def kernel(
    src_ref, order_ref, cell_ref, live_ref, value_ref, error_ref, ocean_ref, weights_ref, atm_ref,
    code_in, move_in, pick_in,
    mean_ref, anom_ref,
    ocn, wts, meta, src, order_in, cell_in, live_in, value_in, error_in,
    tiles_ref, metat_ref, code_ref, move_ref, pick_ref, held, shifted,
    local_sem, send_sem, recv_sem, out_sem,
):
    gx, gy = lax.axis_index("gx"), lax.axis_index("gy")
    nx, ny = lax.axis_size("gx"), lax.axis_size("gy")
    members = tiles_ref.shape[1]
    fields = atm_ref.shape[0]
    cells = tiles_ref.shape[2]
    slots = order_in.shape[1]

    def has_x(dx):
        return (gx + dx >= 0) & (gx + dx < nx)

    def has_y(dy):
        return (gy + dy >= 0) & (gy + dy < ny)

    def there(i):
        return has_x(OFFS[i][0]) & has_y(OFFS[i][1])

    pairs = (
        (ocean_ref, ocn.at[4]), (order_ref, order_in), (cell_ref, cell_in), (live_ref, live_in),
        (value_ref, value_in), (error_ref, error_in), (src_ref, src), (weights_ref, wts),
        (atm_ref, held.at[0:fields]), (code_in, code_ref), (move_in, move_ref), (pick_in, pick_ref),
    )
    staged = [pltpu.make_async_copy(x, y, local_sem.at[n]) for n, (x, y) in enumerate(pairs)]
    for copy in staged:
        copy.start()

    barrier = pltpu.get_barrier_semaphore()
    for i in OTHERS:
        dx, dy = OFFS[i]

        @pl.when(there(i))
        def _():
            pl.semaphore_signal(barrier, inc=1, device_id=(gx + dx, gy + dy), device_id_type=MESH)

    for i in OTHERS:

        @pl.when(jnp.logical_not(there(i)))
        def _():
            tiles_ref[i] = jnp.zeros(tiles_ref.shape[1:], jnp.float32)
            meta[i] = jnp.zeros(meta.shape[1:], jnp.float32)

    for n in range(9, meta.shape[0]):
        meta[n] = jnp.zeros(meta.shape[1:], jnp.float32)

    for copy in staged[1:6]:
        copy.wait()
    cell = cell_in[...]
    spot = ((cell // AY) * CODE + cell % AY).astype(jnp.float32)
    rows = jnp.concatenate(
        [
            spot, value_in[...], error_in[...], live_in[...].astype(jnp.float32),
            jnp.zeros((4, slots), jnp.float32),
        ],
        axis=0,
    )
    slot = lax.broadcasted_iota(jnp.int32, (slots, slots), 0)
    perm = jnp.where(order_in[...] == slot, 1.0, 0.0)
    rows = jnp.dot(rows, perm, precision=lax.Precision.HIGHEST, preferred_element_type=jnp.float32)
    meta[4] = jnp.concatenate([rows, jnp.zeros((8, meta.shape[2] - slots), jnp.float32)], axis=1)

    staged[0].wait()
    across = 1 + has_x(-1).astype(jnp.int32) + has_x(1).astype(jnp.int32)
    along = 1 + has_y(-1).astype(jnp.int32) + has_y(1).astype(jnp.int32)
    pl.semaphore_wait(barrier, across * along - 1)

    outer = lax.rem(gy, 2) * 2 - 1

    def ocean(source, target, n, dx, dy):
        return pltpu.make_async_remote_copy(
            src_ref=ocn.at[source],
            dst_ref=ocn.at[target],
            send_sem=send_sem.at[0, n],
            recv_sem=recv_sem.at[0, target],
            device_id=(gx + dx, gy + dy),
            device_id_type=MESH,
        )

    def arrive(at, dx, dy):
        ocean(at, at, 4, dx, dy).wait_recv()

    firsts = [
        (has_y(outer), ocean(4, 4 - outer, 1, 0, outer)),
        (has_x(-1), ocean(4, 7, 2, -1, 0)),
        (has_x(1), ocean(4, 1, 3, 1, 0)),
        (has_y(-outer), ocean(4, 4 + outer, 0, 0, -outer)),
    ]
    relays = [
        (has_y(outer) & has_x(dx), ocean(4 + outer, 4 - 3 * dx + outer, n, dx, 0))
        for dx, n in ((-1, 5), (1, 6))
    ]
    hands = [
        (dx, has_x(dx) & has_y(-outer), ocean(4 + 3 * dx, 4 + 3 * dx + outer, n, 0, -outer))
        for dx, n in ((-1, 7), (1, 8))
    ]

    def begin(cond, copy):
        @pl.when(cond)
        def _():
            copy.start()

    for cond, copy in firsts:
        begin(cond, copy)

    def remote(buf, kind, i):
        dx, dy = OFFS[i]
        return pltpu.make_async_remote_copy(
            src_ref=buf.at[4],
            dst_ref=buf.at[8 - i],
            send_sem=send_sem.at[kind, i],
            recv_sem=recv_sem.at[kind, 8 - i],
            device_id=(gx + dx, gy + dy),
            device_id_type=MESH,
        )

    def send(buf, kind):
        for i in OTHERS:

            @pl.when(there(i))
            def _():
                remote(buf, kind, i).start()

    def receive(buf, kind):
        for i in OTHERS:

            @pl.when(there(i))
            def _():
                remote(buf, kind, 8 - i).wait_recv()

    def settle(buf, kind):
        for i in OTHERS:

            @pl.when(there(i))
            def _():
                remote(buf, kind, i).wait_send()

    send(meta, 1)

    staged[8].wait()
    for v in range(fields):
        block = held[v]
        mean = jnp.sum(block, axis=0, keepdims=True) / members
        mean_ref[v] = mean
        held[v] = block - mean

    @pl.when(has_y(outer))
    def _():
        arrive(4 + outer, 0, outer)

    for cond, copy in relays:
        begin(cond, copy)
    for dx, cond, copy in hands:

        @pl.when(has_x(dx))
        def _():
            arrive(4 + 3 * dx, dx, 0)

        begin(cond, copy)

    receive(meta, 1)
    flat = meta[...].reshape(meta.shape[0] * meta.shape[1], meta.shape[2])
    metat_ref[...] = flat.T
    staged[6].wait()
    staged[7].wait()
    for copy in staged[9:]:
        copy.wait()

    @pl.when(has_y(-outer))
    def _():
        arrive(4 - outer, 0, -outer)

    for dx in (-1, 1):
        for dy in (outer, -outer):

            @pl.when(has_x(dx) & has_y(dy))
            def _():
                arrive(4 + 3 * dx + dy, dx, 0)

    total = jnp.zeros(tiles_ref.shape[1:], jnp.float32)
    for k in range(wts.shape[0]):
        source = src[0, k]
        position = (source // ny - gx + 1) * 3 + (source % ny - gy + 1)
        position = jnp.clip(position, 0, 8)
        total += jnp.dot(ocn[position], wts[k], preferred_element_type=jnp.float32)
    tiles_ref[4] = total
    send(tiles_ref, 2)
    for cond, copy in firsts + relays + [hand[1:] for hand in hands]:

        @pl.when(cond)
        def _():
            copy.wait_send()

    settle(meta, 1)
    receive(tiles_ref, 2)
    settle(tiles_ref, 2)

    scale = 1.0 / (members - 1)
    beside = split_rows(jnp.concatenate([tiles_ref[i] for i in OTHERS], axis=1))
    halo = jnp.dot(beside, pick_ref[...], preferred_element_type=jnp.float32)
    grid = jnp.concatenate([tiles_ref[4], halo[:members] + halo[members:]], axis=1)
    gmean = jnp.sum(grid, axis=0, keepdims=True) / members
    grid = grid - gmean
    code = code_ref[0:1, :]

    for b in range(NB):
        last = b == NB - 1
        variance = jnp.sum(grid * grid, axis=0, keepdims=True) / (members - 1)
        gains = jnp.zeros((OB, 2 * cells), jnp.float32)
        sums = jnp.zeros((OB, 2 * cells), jnp.float32)
        weights = jnp.zeros((OB, 2 * cells), jnp.float32)
        for i in range(9):
            dx, dy = OFFS[i]
            column = metat_ref[b * OB : (b + 1) * OB, 8 * i : 8 * i + 4]
            spot = column[:, 0:1] + float((AX * dx + AX) * CODE + AY * dy + AY)
            error = column[:, 2:3]
            live = column[:, 3:4]
            denom = variance + (error + (1.0 - live))
            weighting = live / denom
            damping = 1.0 / (1.0 + jnp.sqrt(error / denom))
            hit = spot == code
            weighting = jnp.where(hit, weighting, 0.0)
            weights = weights + weighting
            gains = gains + weighting * damping
            sums = sums + weighting * column[:, 1:2]
        alpha = jnp.sum(gains, axis=0, keepdims=True)
        beta = jnp.sum(sums, axis=0, keepdims=True) - gmean * jnp.sum(weights, axis=0, keepdims=True)
        extra = jnp.concatenate([alpha, beta, jnp.zeros((6, 2 * cells), jnp.float32)], axis=0)
        left = split_rows(jnp.concatenate([grid, extra], axis=0))
        width = (8 if last else 16) * cells
        moved = jnp.dot(left, move_ref[:, :width], preferred_element_type=jnp.float32)
        rows = members + 8
        shifted[:, :width] = moved[:rows] + moved[rows:]

        def step(block, part, center, alpha, beta):
            total = jnp.zeros_like(block)
            mean = jnp.zeros((1, cells), jnp.float32)
            for d in range(9):
                if d == 8:
                    source, a, m = center, alpha * scale, beta * scale
                else:
                    dx, dy = OFFS[OTHERS[d]]
                    weight = scale * taper_of(dx, dy)
                    at = (part * 8 + d) * cells
                    source = shifted[:members, at : at + cells]
                    a = shifted[members : members + 1, at : at + cells] * weight
                    m = shifted[members + 1 : members + 2, at : at + cells] * weight
                cov = jnp.sum(block * source, axis=0, keepdims=True)
                mean = mean + cov * m
                total = total + source * (cov * a)
            return block - total, mean

        own = grid[:, :cells]
        held[fields] = own
        own_args = (alpha[:, :cells], beta[:, :cells])

        def one_field(v, carry, own_args=own_args, last=last, step=step):
            block, mean = step(held[v], 0, held[fields], *own_args)
            held[v] = block
            mean_ref[v] = mean_ref[v] + mean
            if last:
                pltpu.make_async_copy(held.at[v], anom_ref.at[v], out_sem.at[v]).start()
            return carry

        lax.fori_loop(0, fields, one_field, 0)
        block, mean = step(own, 0, own, *own_args)
        if last:
            held[fields] = block
            mean_ref[fields] = gmean[:, :cells] + mean
            pltpu.make_async_copy(
                held.at[fields], anom_ref.at[fields], out_sem.at[fields]
            ).start()
            for v in range(fields + 1):
                pltpu.make_async_copy(held.at[v], anom_ref.at[v], out_sem.at[v]).wait()
        else:
            outer = grid[:, cells:]
            far, far_mean = step(outer, 1, outer, alpha[:, cells:], beta[:, cells:])
            grid = jnp.concatenate([block, far], axis=1)
            gmean = gmean + jnp.concatenate([mean, far_mean], axis=1)


def local(
    atm_members, ocean_members, remap_weights, pair_src, obs_cell, obs_value, obs_error,
    obs_live, obs_order,
):
    members, fields, cells = atm_members.shape[2:]
    slots = obs_cell.shape[2]
    sources, depth = remap_weights.shape[2:4]
    vmem = pl.BlockSpec(memory_space=pltpu.VMEM)
    anywhere = pl.BlockSpec(memory_space=pl.ANY)
    code, move, pick = tables()
    post_mean, post_anom = pl.pallas_call(
        kernel,
        out_shape=(
            jax.ShapeDtypeStruct((fields + 1, 1, cells), jnp.float32),
            jax.ShapeDtypeStruct((fields + 1, members, cells), jnp.float32),
        ),
        in_specs=[anywhere] * 12,
        out_specs=(vmem, anywhere),
        scratch_shapes=[
            pltpu.VMEM((9, members, depth), jnp.bfloat16),
            pltpu.VMEM((sources, depth, cells), jnp.bfloat16),
            pltpu.VMEM((16, 8, 128), jnp.float32),
            pltpu.SMEM((1, sources), jnp.int32),
            pltpu.VMEM((1, slots), jnp.int32),
            pltpu.VMEM((1, slots), jnp.int32),
            pltpu.VMEM((1, slots), jnp.int32),
            pltpu.VMEM((1, slots), jnp.float32),
            pltpu.VMEM((1, slots), jnp.float32),
            pltpu.VMEM((9, members, cells), jnp.float32),
            pltpu.VMEM((128, 128), jnp.float32),
            pltpu.VMEM(code.shape, jnp.float32),
            pltpu.VMEM(move.shape, jnp.bfloat16),
            pltpu.VMEM(pick.shape, jnp.bfloat16),
            pltpu.VMEM((fields + 1, members, cells), jnp.float32),
            pltpu.VMEM((members + 8, 16 * cells), jnp.float32),
            pltpu.SemaphoreType.DMA((12,)),
            pltpu.SemaphoreType.DMA((3, 9)),
            pltpu.SemaphoreType.DMA((3, 9)),
            pltpu.SemaphoreType.DMA((fields + 1,)),
        ],
        compiler_params=pltpu.CompilerParams(
            collective_id=0, has_side_effects=True, vmem_limit_bytes=LIMIT
        ),
        name="fused",
    )(
        pair_src[0], obs_order[0], obs_cell[0], obs_live[0], obs_value[0], obs_error[0],
        ocean_members[0, 0], remap_weights[0, 0], jnp.transpose(atm_members[0, 0], (1, 0, 2)),
        jnp.asarray(code), jnp.asarray(move, jnp.bfloat16), jnp.asarray(pick, jnp.bfloat16),
    )
    return (post_mean.reshape(1, 1, fields + 1, cells), jnp.transpose(post_anom, (1, 0, 2))[None, None])


def solution(mesh):
    in_specs = (
        P("gx", "gy", None, None, None),
        P("gx", "gy", None, None),
        P("gx", "gy", None, None, None),
        P("gx", "gy", None),
        P("gx", "gy", None),
        P("gx", "gy", None),
        P("gx", "gy", None),
        P("gx", "gy", None),
        P("gx", "gy", None),
    )
    out_specs = (P("gx", "gy", None, None), P("gx", "gy", None, None, None))
    return jax.shard_map(local, mesh=mesh, in_specs=in_specs, out_specs=out_specs, check_vma=False)
```

time: 35.5 us -> 27.3 us (0.77)
  the two profiles are of different devices: /device:TPU:4 before, /device:TPU:3 now
where the time goes in v2:
time: 27.3 us; the launch traced here: 27.1 us
  Pallas kernels  23.3 us (85%)
  local copies, waits for them, and re-layouts  3.15 us (12%)
  between operations  0.65 us (2%)
    pallas_call x1, Pallas kernels, local(): pl.pallas_call(kernel, out_shape=(jax.ShapeDtypeStruct((fields + 1, 1, ce...  23.3 us
    unnamed x4, local copies, waits for them, and re-layouts  3.15 us

profile of v2, /device:TPU:3, one launch (start us, length us, event | category | flops | bytes accessed | tf_op | source)
XLA Modules:
  0.0 27.1 jit_solution(7098023393265519559)
XLA Ops:
  0.6 23.3 %fused.1 = (f32[13,1,128]{2,1,0:T(1,128)}, f32[13,80,128]{2,1,0:T(8,128)}) custom-call(s32[1,4]{1,0:T(1,128)} %bitcast.22, s32[1,64]{1,0:T(1,128)} %bitcast.23, s32[1,64]{1,0:T(1,128)} %bitcast.24, s32[1,64]{1,0:T(1,128)} %bitcast.25, f32[1,64]{1,0:T(1,128)} %bitcast.26, f32[1,64]{1,0:T(1,128)} %bitcast.27, bf16[80,1024]{1,0:T(8,128)(2,1)} %bitcast.20, ...), custom_call_target="tpu_custom_call" | custom-call | tf_op jit(solution)/shard_map/fused/pallas_call | solution.py:358
  23.9 0.0 copy-start
  23.9 0.7 %copy-done = f32[13,1,128]{2,1,0:T(1,128)S(1)} copy-done((f32[13,1,128]{2,1,0:T(1,128)S(1)}, f32[13,1,128]{2,1,0:T(1,128)}, u32[]{:S(2)}) %copy-start) | copy-done | bytes 6680
  24.6 0.6 %copy.17 = f32[1,1,13,128]{3,1,2,0:T(1,128)} copy(f32[1,1,13,128]{3,1,2,0:T(1,128)S(1)} %bitcast.21) | data formatting | bytes 13312
  25.2 1.9 %copy.18 = f32[1,1,80,13,128]{4,2,3,1,0:T(8,128)} copy(f32[1,1,80,13,128]{4,2,3,1,0:T(8,128)} %bitcast.18) | data formatting | bytes 1064960
Async XLA Ops:
  23.9 0.7 %copy-start = (f32[13,1,128]{2,1,0:T(1,128)S(1)}, f32[13,1,128]{2,1,0:T(1,128)}, u32[]{:S(2)}) copy-start(f32[13,1,128]{2,1,0:T(1,128)} %get-tuple-element.4) | copy-start | bytes 19972

commit v3 on v2

--- a/solution.py
+++ b/solution.py
@@ -14,7 +14,7 @@
 NB = 2
 RAD = 2
 CODE = 64
-LIMIT = 66977792
+LIMIT = 65400 * 1024
 
 MESH = pl.DeviceIdType.MESH
 OFFS = [(dx, dy) for dx in (-1, 0, 1) for dy in (-1, 0, 1)]
@@ -59,19 +59,17 @@
     return jnp.concatenate([high, block - high], axis=0).astype(jnp.bfloat16)
 
 
-def kernel(
+def exchange_kernel(
     src_ref, order_ref, cell_ref, live_ref, value_ref, error_ref, ocean_ref, weights_ref, atm_ref,
-    code_in, move_in, pick_in,
-    mean_ref, anom_ref,
+    tiles_ref, metat_ref, fields_ref, fmean_ref,
     ocn, wts, meta, src, order_in, cell_in, live_in, value_in, error_in,
-    tiles_ref, metat_ref, code_ref, move_ref, pick_ref, held, shifted,
+    own, blank, metat, held, fmean,
     local_sem, send_sem, recv_sem, out_sem,
 ):
     gx, gy = lax.axis_index("gx"), lax.axis_index("gy")
     nx, ny = lax.axis_size("gx"), lax.axis_size("gy")
     members = tiles_ref.shape[1]
     fields = atm_ref.shape[0]
-    cells = tiles_ref.shape[2]
     slots = order_in.shape[1]
 
     def has_x(dx):
@@ -86,12 +84,13 @@
     pairs = (
         (ocean_ref, ocn.at[4]), (order_ref, order_in), (cell_ref, cell_in), (live_ref, live_in),
         (value_ref, value_in), (error_ref, error_in), (src_ref, src), (weights_ref, wts),
-        (atm_ref, held.at[0:fields]), (code_in, code_ref), (move_in, move_ref), (pick_in, pick_ref),
+        (atm_ref, held),
     )
     staged = [pltpu.make_async_copy(x, y, local_sem.at[n]) for n, (x, y) in enumerate(pairs)]
     for copy in staged:
         copy.start()
 
+    blank[...] = jnp.zeros(blank.shape, jnp.float32)
     barrier = pltpu.get_barrier_semaphore()
     for i in OTHERS:
         dx, dy = OFFS[i]
@@ -104,7 +103,7 @@
 
         @pl.when(jnp.logical_not(there(i)))
         def _():
-            tiles_ref[i] = jnp.zeros(tiles_ref.shape[1:], jnp.float32)
+            pltpu.make_async_copy(blank, tiles_ref.at[i], out_sem.at[i]).start()
             meta[i] = jnp.zeros(meta.shape[1:], jnp.float32)
 
     for n in range(9, meta.shape[0]):
@@ -180,6 +179,17 @@
             device_id_type=MESH,
         )
 
+    def column(i):
+        dx, dy = OFFS[i]
+        return pltpu.make_async_remote_copy(
+            src_ref=own,
+            dst_ref=tiles_ref.at[8 - i],
+            send_sem=send_sem.at[2, i],
+            recv_sem=recv_sem.at[2, 8 - i],
+            device_id=(gx + dx, gy + dy),
+            device_id_type=MESH,
+        )
+
     def send(buf, kind):
         for i in OTHERS:
 
@@ -207,8 +217,16 @@
     for v in range(fields):
         block = held[v]
         mean = jnp.sum(block, axis=0, keepdims=True) / members
-        mean_ref[v] = mean
+        fmean[v : v + 1, :] = mean
         held[v] = block - mean
+    results = [
+        pltpu.make_async_copy(held, fields_ref, local_sem.at[9]),
+        pltpu.make_async_copy(fmean, fmean_ref, local_sem.at[10]),
+        pltpu.make_async_copy(metat, metat_ref, local_sem.at[11]),
+        pltpu.make_async_copy(own, tiles_ref.at[4], out_sem.at[4]),
+    ]
+    results[0].start()
+    results[1].start()
 
     @pl.when(has_y(outer))
     def _():
@@ -226,11 +244,10 @@
 
     receive(meta, 1)
     flat = meta[...].reshape(meta.shape[0] * meta.shape[1], meta.shape[2])
-    metat_ref[...] = flat.T
+    metat[...] = flat.T
+    results[2].start()
     staged[6].wait()
     staged[7].wait()
-    for copy in staged[9:]:
-        copy.wait()
 
     @pl.when(has_y(-outer))
     def _():
@@ -249,8 +266,14 @@
         position = (source // ny - gx + 1) * 3 + (source % ny - gy + 1)
         position = jnp.clip(position, 0, 8)
         total += jnp.dot(ocn[position], wts[k], preferred_element_type=jnp.float32)
-    tiles_ref[4] = total
-    send(tiles_ref, 2)
+    own[...] = total
+    for i in OTHERS:
+
+        @pl.when(there(i))
+        def _():
+            column(i).start()
+
+    results[3].start()
     for cond, copy in firsts + relays + [hand[1:] for hand in hands]:
 
         @pl.when(cond)
@@ -258,8 +281,36 @@
             copy.wait_send()
 
     settle(meta, 1)
-    receive(tiles_ref, 2)
-    settle(tiles_ref, 2)
+    for copy in results:
+        copy.wait()
+    for i in OTHERS:
+
+        @pl.when(jnp.logical_not(there(i)))
+        def _():
+            pltpu.make_async_copy(blank, tiles_ref.at[i], out_sem.at[i]).wait()
+
+        @pl.when(there(i))
+        def _():
+            column(i).wait_send()
+            column(8 - i).wait_recv()
+
+
+def analysis_kernel(
+    tiles_in, metat_in, fields_in, fmean_in, code_in, move_in, pick_in,
+    mean_ref, anom_ref,
+    tiles_ref, metat_ref, fmean_ref, code_ref, move_ref, pick_ref, held, shifted, local_sem, out_sem,
+):
+    fields, members, cells = fields_in.shape
+    pairs = (
+        (tiles_in, tiles_ref), (metat_in, metat_ref), (fmean_in, fmean_ref),
+        (fields_in, held.at[0:fields]), (pick_in, pick_ref), (code_in, code_ref),
+        (move_in, move_ref),
+    )
+    staged = [pltpu.make_async_copy(x, y, local_sem.at[n]) for n, (x, y) in enumerate(pairs)]
+    for n in (0, 4, 1, 5, 6, 2, 3):
+        staged[n].start()
+    staged[0].wait()
+    staged[4].wait()
 
     scale = 1.0 / (members - 1)
     beside = split_rows(jnp.concatenate([tiles_ref[i] for i in OTHERS], axis=1))
@@ -267,6 +318,8 @@
     grid = jnp.concatenate([tiles_ref[4], halo[:members] + halo[members:]], axis=1)
     gmean = jnp.sum(grid, axis=0, keepdims=True) / members
     grid = grid - gmean
+    staged[1].wait()
+    staged[5].wait()
     code = code_ref[0:1, :]
 
     for b in range(NB):
@@ -292,6 +345,8 @@
         alpha = jnp.sum(gains, axis=0, keepdims=True)
         beta = jnp.sum(sums, axis=0, keepdims=True) - gmean * jnp.sum(weights, axis=0, keepdims=True)
         extra = jnp.concatenate([alpha, beta, jnp.zeros((6, 2 * cells), jnp.float32)], axis=0)
+        if b == 0:
+            staged[6].wait()
         left = split_rows(jnp.concatenate([grid, extra], axis=0))
         width = (8 if last else 16) * cells
         moved = jnp.dot(left, move_ref[:, :width], preferred_element_type=jnp.float32)
@@ -318,12 +373,16 @@
 
         own = grid[:, :cells]
         held[fields] = own
+        if b == 0:
+            staged[2].wait()
+            staged[3].wait()
         own_args = (alpha[:, :cells], beta[:, :cells])
 
-        def one_field(v, carry, own_args=own_args, last=last, step=step):
+        def one_field(v, carry, own_args=own_args, last=last, b=b, step=step):
             block, mean = step(held[v], 0, held[fields], *own_args)
             held[v] = block
-            mean_ref[v] = mean_ref[v] + mean
+            before = fmean_ref[pl.ds(v, 1), :] if b == 0 else mean_ref[v]
+            mean_ref[v] = before + mean
             if last:
                 pltpu.make_async_copy(held.at[v], anom_ref.at[v], out_sem.at[v]).start()
             return carry
@@ -355,14 +414,17 @@
     vmem = pl.BlockSpec(memory_space=pltpu.VMEM)
     anywhere = pl.BlockSpec(memory_space=pl.ANY)
     code, move, pick = tables()
-    post_mean, post_anom = pl.pallas_call(
-        kernel,
-        out_shape=(
-            jax.ShapeDtypeStruct((fields + 1, 1, cells), jnp.float32),
-            jax.ShapeDtypeStruct((fields + 1, members, cells), jnp.float32),
-        ),
-        in_specs=[anywhere] * 12,
-        out_specs=(vmem, anywhere),
+    results = (
+        jax.ShapeDtypeStruct((9, members, cells), jnp.float32),
+        jax.ShapeDtypeStruct((128, 128), jnp.float32),
+        jax.ShapeDtypeStruct((fields, members, cells), jnp.float32),
+        jax.ShapeDtypeStruct((fields, cells), jnp.float32),
+    )
+    state = pl.pallas_call(
+        exchange_kernel,
+        out_shape=results,
+        in_specs=[anywhere] * 9,
+        out_specs=(anywhere,) * 4,
         scratch_shapes=[
             pltpu.VMEM((9, members, depth), jnp.bfloat16),
             pltpu.VMEM((sources, depth, cells), jnp.bfloat16),
@@ -373,27 +435,45 @@
             pltpu.VMEM((1, slots), jnp.int32),
             pltpu.VMEM((1, slots), jnp.float32),
             pltpu.VMEM((1, slots), jnp.float32),
-            pltpu.VMEM((9, members, cells), jnp.float32),
+            pltpu.VMEM((members, cells), jnp.float32),
+            pltpu.VMEM((members, cells), jnp.float32),
             pltpu.VMEM((128, 128), jnp.float32),
+            pltpu.VMEM((fields, members, cells), jnp.float32),
+            pltpu.VMEM((fields, cells), jnp.float32),
+            pltpu.SemaphoreType.DMA((12,)),
+            pltpu.SemaphoreType.DMA((3, 9)),
+            pltpu.SemaphoreType.DMA((3, 9)),
+            pltpu.SemaphoreType.DMA((9,)),
+        ],
+        compiler_params=pltpu.CompilerParams(
+            collective_id=0, has_side_effects=True, vmem_limit_bytes=LIMIT
+        ),
+        name="exchange",
+    )(
+        pair_src[0], obs_order[0], obs_cell[0], obs_live[0], obs_value[0], obs_error[0],
+        ocean_members[0, 0], remap_weights[0, 0], jnp.transpose(atm_members[0, 0], (1, 0, 2)),
+    )
+    post_mean, post_anom = pl.pallas_call(
+        analysis_kernel,
+        out_shape=(
+            jax.ShapeDtypeStruct((fields + 1, 1, cells), jnp.float32),
+            jax.ShapeDtypeStruct((fields + 1, members, cells), jnp.float32),
+        ),
+        in_specs=[anywhere] * 7,
+        out_specs=(vmem, anywhere),
+        scratch_shapes=[
+            *(pltpu.VMEM(r.shape, jnp.float32) for r in (results[0], results[1], results[3])),
             pltpu.VMEM(code.shape, jnp.float32),
             pltpu.VMEM(move.shape, jnp.bfloat16),
             pltpu.VMEM(pick.shape, jnp.bfloat16),
             pltpu.VMEM((fields + 1, members, cells), jnp.float32),
             pltpu.VMEM((members + 8, 16 * cells), jnp.float32),
-            pltpu.SemaphoreType.DMA((12,)),
-            pltpu.SemaphoreType.DMA((3, 9)),
-            pltpu.SemaphoreType.DMA((3, 9)),
+            pltpu.SemaphoreType.DMA((7,)),
             pltpu.SemaphoreType.DMA((fields + 1,)),
         ],
-        compiler_params=pltpu.CompilerParams(
-            collective_id=0, has_side_effects=True, vmem_limit_bytes=LIMIT
-        ),
-        name="fused",
-    )(
-        pair_src[0], obs_order[0], obs_cell[0], obs_live[0], obs_value[0], obs_error[0],
-        ocean_members[0, 0], remap_weights[0, 0], jnp.transpose(atm_members[0, 0], (1, 0, 2)),
-        jnp.asarray(code), jnp.asarray(move, jnp.bfloat16), jnp.asarray(pick, jnp.bfloat16),
-    )
+        compiler_params=pltpu.CompilerParams(vmem_limit_bytes=LIMIT),
+        name="analysis",
+    )(*state, jnp.asarray(code), jnp.asarray(move, jnp.bfloat16), jnp.asarray(pick, jnp.bfloat16))
     return (post_mean.reshape(1, 1, fields + 1, cells), jnp.transpose(post_anom, (1, 0, 2))[None, None])
 
 

time: 27.3 us -> 25.5 us (0.934)
  local copies, waits for them, and re-layouts: 3.15 us -> 0 us
  Pallas kernels: 23.3 us -> 24.8 us
    unnamed x4 -> x0, local copies, waits for them, and re-layouts: 3.15 us -> none
    pallas_call x1 -> x2, Pallas kernels: 23.3 us -> 24.8 us  [the longest x1 19 us: local(): pl.pallas_call(exchange_kernel, out_shape=results, in_specs=[anywhere] *...]
where the time goes in v3:
time: 25.5 us; the launch traced here: 25.4 us
  Pallas kernels  24.8 us (97%)
  between operations  0.64 us (3%)
    pallas_call x1, Pallas kernels, local(): pl.pallas_call(exchange_kernel, out_shape=results, in_specs=[anywhere] *...  19 us
    pallas_call x1, Pallas kernels, local(): pl.pallas_call(analysis_kernel, out_shape=(jax.ShapeDtypeStruct((fields +...  5.77 us

profile of v3, /device:TPU:3, one launch (start us, length us, event | category | flops | bytes accessed | tf_op | source)
XLA Modules:
  0.0 25.4 jit_solution(14812812128867045136)
XLA Ops:
  0.6 19.0 %exchange.1 = (f32[9,80,128]{2,1,0:T(8,128)}, f32[128,128]{1,0:T(8,128)}, f32[12,80,128]{2,1,0:T(8,128)}, f32[12,128]{1,0:T(8,128)}) custom-call(s32[1,4]{1,0:T(1,128)} %bitcast.20, s32[1,64]{1,0:T(1,128)} %bitcast.21, s32[1,64]{1,0:T(1,128)} %bitcast.22, s32[1,64]{1,0:T(1,128)} %bitcast.23, f32[1,64]{1,0:T(1,128)} %bitcast.24, f32[1,64]{1,0:T(1,128)} %bitcast.25, ...), custom_call_target="tpu_custom_call" | custom-call | tf_op jit(solution)/shard_map/exchange/pallas_call | solution.py:423
  19.6 5.8 %analysis.1 = (f32[13,1,128]{2,1,0:T(1,128)}, f32[13,80,128]{2,1,0:T(8,128)}) custom-call(f32[9,80,128]{2,1,0:T(8,128)} %get-tuple-element.8.tiles_in, f32[128,128]{1,0:T(8,128)} %get-tuple-element.9.metat_in, f32[12,80,128]{2,1,0:T(8,128)} %get-tuple-element.10.fields_in, f32[12,128]{1,0:T(8,128)} %get-tuple-element.11.fmean_in, ...), custom_call_target="tpu_custom_call" | custom-call | tf_op jit(solution)/shard_map/analysis/pallas_call | solution.py:456

commit v4 on v3

--- a/solution.py
+++ b/solution.py
@@ -132,31 +132,44 @@
 
     outer = lax.rem(gy, 2) * 2 - 1
 
-    def ocean(source, target, n, dx, dy):
+    first = (members // 2 + 15) // 16 * 16
+    parts = ((0, 0, first), (3, first, members - first))
+
+    def ocean(part, source, target, n, dx, dy):
+        kind, low, size = part
         return pltpu.make_async_remote_copy(
-            src_ref=ocn.at[source],
-            dst_ref=ocn.at[target],
-            send_sem=send_sem.at[0, n],
-            recv_sem=recv_sem.at[0, target],
+            src_ref=ocn.at[source, pl.ds(low, size)],
+            dst_ref=ocn.at[target, pl.ds(low, size)],
+            send_sem=send_sem.at[kind, n],
+            recv_sem=recv_sem.at[kind, target],
             device_id=(gx + dx, gy + dy),
             device_id_type=MESH,
         )
 
-    def arrive(at, dx, dy):
-        ocean(at, at, 4, dx, dy).wait_recv()
+    def arrive(part, at, dx, dy):
+        ocean(part, at, at, 4, dx, dy).wait_recv()
 
     firsts = [
-        (has_y(outer), ocean(4, 4 - outer, 1, 0, outer)),
-        (has_x(-1), ocean(4, 7, 2, -1, 0)),
-        (has_x(1), ocean(4, 1, 3, 1, 0)),
-        (has_y(-outer), ocean(4, 4 + outer, 0, 0, -outer)),
+        (cond, ocean(part, 4, target, n, dx, dy))
+        for part in parts
+        for cond, target, n, dx, dy in (
+            (has_y(outer), 4 - outer, 1, 0, outer),
+            (has_x(-1), 7, 2, -1, 0),
+            (has_x(1), 1, 3, 1, 0),
+            (has_y(-outer), 4 + outer, 0, 0, -outer),
+        )
     ]
     relays = [
-        (has_y(outer) & has_x(dx), ocean(4 + outer, 4 - 3 * dx + outer, n, dx, 0))
+        (has_y(outer) & has_x(dx), ocean(part, 4 + outer, 4 - 3 * dx + outer, n, dx, 0))
+        for part in parts
         for dx, n in ((-1, 5), (1, 6))
     ]
     hands = [
-        (dx, has_x(dx) & has_y(-outer), ocean(4 + 3 * dx, 4 + 3 * dx + outer, n, 0, -outer))
+        (
+            part, dx, has_x(dx) & has_y(-outer),
+            ocean(part, 4 + 3 * dx, 4 + 3 * dx + outer, n, 0, -outer),
+        )
+        for part in parts
         for dx, n in ((-1, 7), (1, 8))
     ]
 
@@ -228,17 +241,19 @@
     results[0].start()
     results[1].start()
 
-    @pl.when(has_y(outer))
-    def _():
-        arrive(4 + outer, 0, outer)
-
-    for cond, copy in relays:
-        begin(cond, copy)
-    for dx, cond, copy in hands:
+    for at, part in enumerate(parts):
+
+        @pl.when(has_y(outer))
+        def _():
+            arrive(part, 4 + outer, 0, outer)
+
+        for cond, copy in relays[2 * at : 2 * at + 2]:
+            begin(cond, copy)
+    for part, dx, cond, copy in hands:
 
         @pl.when(has_x(dx))
         def _():
-            arrive(4 + 3 * dx, dx, 0)
+            arrive(part, 4 + 3 * dx, dx, 0)
 
         begin(cond, copy)
 
@@ -249,16 +264,18 @@
     staged[6].wait()
     staged[7].wait()
 
-    @pl.when(has_y(-outer))
-    def _():
-        arrive(4 - outer, 0, -outer)
-
-    for dx in (-1, 1):
-        for dy in (outer, -outer):
-
-            @pl.when(has_x(dx) & has_y(dy))
-            def _():
-                arrive(4 + 3 * dx + dy, dx, 0)
+    for part in parts:
+
+        @pl.when(has_y(-outer))
+        def _():
+            arrive(part, 4 - outer, 0, -outer)
+
+        for dx in (-1, 1):
+            for dy in (outer, -outer):
+
+                @pl.when(has_x(dx) & has_y(dy))
+                def _():
+                    arrive(part, 4 + 3 * dx + dy, dx, 0)
 
     total = jnp.zeros(tiles_ref.shape[1:], jnp.float32)
     for k in range(wts.shape[0]):
@@ -274,7 +291,7 @@
             column(i).start()
 
     results[3].start()
-    for cond, copy in firsts + relays + [hand[1:] for hand in hands]:
+    for cond, copy in firsts + relays + [hand[2:] for hand in hands]:
 
         @pl.when(cond)
         def _():
@@ -441,8 +458,8 @@
             pltpu.VMEM((fields, members, cells), jnp.float32),
             pltpu.VMEM((fields, cells), jnp.float32),
             pltpu.SemaphoreType.DMA((12,)),
-            pltpu.SemaphoreType.DMA((3, 9)),
-            pltpu.SemaphoreType.DMA((3, 9)),
+            pltpu.SemaphoreType.DMA((4, 9)),
+            pltpu.SemaphoreType.DMA((4, 9)),
             pltpu.SemaphoreType.DMA((9,)),
         ],
         compiler_params=pltpu.CompilerParams(

time: 25.5 us -> 25.5 us (level)
  the two profiles are of different devices: /device:TPU:3 before, /device:TPU:4 now
where the time goes in v4:
time: 25.5 us; the launch traced here: 25.4 us
  Pallas kernels  24.7 us (97%)
  between operations  0.64 us (3%)
    pallas_call x1, Pallas kernels, local(): pl.pallas_call(exchange_kernel, out_shape=results, in_specs=[anywhere] *...  19 us
    pallas_call x1, Pallas kernels, local(): pl.pallas_call(analysis_kernel, out_shape=(jax.ShapeDtypeStruct((fields +...  5.77 us

profile of v4, /device:TPU:4, one launch (start us, length us, event | category | flops | bytes accessed | tf_op | source)
XLA Modules:
  0.0 25.4 jit_solution(10450968239643205221)
XLA Ops:
  0.6 19.0 %exchange.1 = (f32[9,80,128]{2,1,0:T(8,128)}, f32[128,128]{1,0:T(8,128)}, f32[12,80,128]{2,1,0:T(8,128)}, f32[12,128]{1,0:T(8,128)}) custom-call(s32[1,4]{1,0:T(1,128)} %bitcast.20, s32[1,64]{1,0:T(1,128)} %bitcast.21, s32[1,64]{1,0:T(1,128)} %bitcast.22, s32[1,64]{1,0:T(1,128)} %bitcast.23, f32[1,64]{1,0:T(1,128)} %bitcast.24, f32[1,64]{1,0:T(1,128)} %bitcast.25, ...), custom_call_target="tpu_custom_call" | custom-call | tf_op jit(solution)/shard_map/exchange/pallas_call | solution.py:440
  19.6 5.8 %analysis.1 = (f32[13,1,128]{2,1,0:T(1,128)}, f32[13,80,128]{2,1,0:T(8,128)}) custom-call(f32[9,80,128]{2,1,0:T(8,128)} %get-tuple-element.8.tiles_in, f32[128,128]{1,0:T(8,128)} %get-tuple-element.9.metat_in, f32[12,80,128]{2,1,0:T(8,128)} %get-tuple-element.10.fields_in, f32[12,128]{1,0:T(8,128)} %get-tuple-element.11.fmean_in, ...), custom_call_target="tpu_custom_call" | custom-call | tf_op jit(solution)/shard_map/analysis/pallas_call | solution.py:473
